TPU v7x, 32 devices: a whole 2x2x4 slice. The times are simulated.
32 devices in a mesh: gx: 2 (over y), gy: 4 (over z), gz: 4 (over x, core).
Axes of the slice: x: 2, y: 2, z: 4, core: 2. Of those that a mesh axis runs over, the one named last changes fastest.
Arguments:
- gas_temp: float32 [128, 128, 1024], P('gz', 'gx', 'gy'), may hold values from 1 to 8
- fuel_frac: float32 [128, 128, 1024], P('gz', 'gx', 'gy'), may hold values from 0 to 1
- velocity: float32 [3, 128, 128, 1024], P(None, 'gz', 'gx', 'gy'), may hold values from -3 to 3
- wall_flags: int32 [128, 1024], P('gx', 'gy'), may hold values 0 or 1
- solid_temp: float32 [64, 256, 2048], P(None, ('gx', 'gy'), 'gz'), may hold values from 1 to 3
- diffusivity: float32 [64, 256, 2048], P(None, ('gx', 'gy'), 'gz'), may hold values from 0.03 to 0.15
- gas_owner: int32 [256, 2048], P(('gx', 'gy'), 'gz'), may hold values from 0 to 131071, as said below
Outputs:
- gas_temp_new: float32 [128, 128, 1024], P('gz', 'gx', 'gy')
- fuel_frac_new: float32 [128, 128, 1024], P('gz', 'gx', 'gy')
- solid_temp_new: float32 [64, 256, 2048], P(None, ('gx', 'gy'), 'gz')
Inputs may be any that keep to these rules, and one draw needn't show every extreme that they name: gas_owner[p, q] = a * 1024 + b where a differs from p // 2 by at most 4 modulo 128 and b differs from q // 2 by at most 4 modulo 1024; both offsets reach 4 in both directions.
All inputs are finite; a program needn't handle non-finite values. No bound on the sum of `wall_flags` on one device may be relied on, other than what follows from the above.
Results may differ from a plain program's by a relative error of at most 0.00002.
Values sent between devices are 32-bit elements; how exact they have to be, the bound alone decides.
A program may use at most 128 MiB of HBM per device.

v0:
```python
import functools

import jax
import jax.numpy as jnp
from jax import lax
from jax.experimental import pallas as pl
from jax.experimental.pallas import tpu as pltpu
from jax.sharding import PartitionSpec as P

SUBSTEPS = 4
DISP = 4

FILM_COEF = 0.15
SOURCE_GAIN = 0.25
COOLANT = 1.0
DIFFUSE_TEMP = 0.2
DIFFUSE_FUEL = 0.15
TIME_STEP = 0.2
RATE_CONST = 1.0
ACTIVATION = 4.0
HEAT_RELEASE = 3.0

LANES = 128
HALO = SUBSTEPS
REACH = DISP + HALO // 2
SPAN = 2 * DISP + 1
HIGHEST = lax.Precision.HIGHEST
VMEM = pl.BlockSpec(memory_space=pltpu.VMEM)


def iota(shape, dim):
    return lax.broadcasted_iota(jnp.int32, shape, dim)


def shift_pairs(count):
    forward = [(i, (i + 1) % count) for i in range(count)]
    return forward, [(b, a) for a, b in forward]


def exchange(first, last, axis):
    forward, backward = shift_pairs(lax.axis_size(axis))
    return lax.ppermute(first, axis, backward), lax.ppermute(last, axis, forward)


def pack_kernel(temp_lo, temp_hi, fuel_lo, fuel_hi, s_lo, s_hi, d_lo, d_hi, c_lo, c_hi, gas_out, wall_out):
    nz, rows, _ = temp_lo.shape
    layers, wrows, _ = s_lo.shape
    per = LANES // HALO
    lane = iota((rows, LANES), 1)

    def gas_body(z, acc):
        low, high = acc
        for f, (lo, hi) in enumerate(((temp_lo, temp_hi), (fuel_lo, fuel_hi))):
            k = f * nz + z
            low = jnp.where(lane == k, pltpu.roll(lo[z], k, 1), low)
            high = jnp.where(lane == k, pltpu.roll(hi[z], k + 1, 1), high)
        return low, high

    zero = jnp.zeros((rows, LANES), jnp.float32)
    low, high = lax.fori_loop(0, nz, gas_body, (zero, zero))
    gas_out[0] = low
    gas_out[1] = high

    group_of = iota((wrows, LANES), 1) // HALO
    groups = layers // per
    wzero = jnp.zeros((wrows, LANES), jnp.float32)
    for g in range(groups):

        def wall_body(k, acc):
            out = []
            for n, ref in enumerate((s_lo, s_hi, d_lo, d_hi)):
                shift = HALO * k if n % 2 == 0 else lax.rem(HALO * k + HALO, LANES)
                out.append(jnp.where(group_of == k, pltpu.roll(ref[g * per + k], shift, 1), acc[n]))
            return tuple(out)

        packed = lax.fori_loop(0, per, wall_body, (wzero,) * 4)
        wall_out[0, g] = packed[0]
        wall_out[1, g] = packed[1]
        wall_out[0, groups + g] = packed[2]
        wall_out[1, groups + g] = packed[3]
    wall_out[0, 2 * groups] = c_lo[...]
    wall_out[1, 2 * groups] = pltpu.roll(c_hi[...], HALO, 1)


def gas_kernel(step_layers, temp, fuel, vel, x_low, x_high, y_low, y_high, z_low, z_high, temp_out, fuel_out):
    nz, rows, cols = temp.shape
    base = pl.program_id(0) * step_layers
    row = iota((rows, cols), 0)
    col = iota((rows, cols), 1)
    tiles = cols // LANES

    def wide(x):
        return jnp.concatenate([x] * tiles, axis=1)

    for i in range(step_layers):
        z = base + i
        centers = (temp[z], fuel[z])
        reaction = RATE_CONST * centers[1] * jnp.exp(-ACTIVATION / centers[0])
        for f, ref in enumerate((temp, fuel)):
            c = centers[f]
            if i == 0:
                below = jnp.where(z == 0, z_low[f], ref[jnp.maximum(z - 1, 0)])
            else:
                below = ref[z - 1]
            if i == step_layers - 1:
                above = jnp.where(z == nz - 1, z_high[f], ref[jnp.minimum(z + 1, nz - 1)])
            else:
                above = ref[z + 1]
            xl = jnp.where(row == 0, x_low[f, pl.ds(z, 1), :], pltpu.roll(c, 1, 0))
            xh = jnp.where(row == rows - 1, x_high[f, pl.ds(z, 1), :], pltpu.roll(c, rows - 1, 0))
            k = f * nz + z
            edge_l = wide(pltpu.roll(y_low[...], LANES - k, 1))
            edge_h = wide(pltpu.roll(y_high[...], LANES - 1 - k, 1))
            yl = jnp.where(col == 0, edge_l, pltpu.roll(c, 1, 1))
            yh = jnp.where(col == cols - 1, edge_h, pltpu.roll(c, cols - 1, 1))
            advect = 0.5 * (vel[0, i] * (above - below) + vel[1, i] * (xh - xl) + vel[2, i] * (yh - yl))
            nearby = below + above + xl + xh + yl + yh
            if f == 0:
                rate = -advect + DIFFUSE_TEMP * (nearby - 6.0 * c) + HEAT_RELEASE * reaction
                temp_out[i] = c + TIME_STEP * rate
            else:
                rate = -advect + DIFFUSE_FUEL * (nearby - 6.0 * c) - reaction
                fuel_out[i] = c + TIME_STEP * rate


def wall_kernel(s, d, code, after, before, packs, face, s_out, tile_out, a, b, dd, code_s, gas_s, film_s, up_s, flux_s):
    layers, rows, cols = s.shape
    ext_r, ext_c = a.shape[1:]
    up_r = up_s.shape[1]
    per = LANES // HALO
    groups = layers // per
    lane = iota((ext_r, LANES), 1)

    def fill(dst, z, src, layer, group, k):
        dst[z, 0:rows, 0:cols] = src[z]
        dst[z, rows : rows + HALO, 0:cols] = after[layer]
        dst[z, rows + HALO : rows + 2 * HALO, 0:cols] = before[layer]
        right = pltpu.roll(packs[0, group], LANES - HALO * k, 1)
        left = pltpu.roll(packs[1, group], LANES - HALO - HALO * k, 1)
        dst[z, :, cols:] = jnp.where(lane < LANES // 2, right, left)

    for g in range(groups):

        def fill_body(k, carry):
            z = g * per + k
            fill(a, z, s, z, g, k)
            fill(dd, z, d, layers + z, groups + g, k)
            return carry

        lax.fori_loop(0, per, fill_body, 0)
    a[layers] = jnp.full((ext_r, ext_c), COOLANT, jnp.float32)
    b[layers] = jnp.full((ext_r, ext_c), COOLANT, jnp.float32)

    code_s[...] = jnp.full((up_r, ext_c), -1.0, jnp.float32)
    code_s[0:rows, 0:cols] = code[...]
    code_s[rows : rows + HALO, 0:cols] = after[2 * layers]
    code_s[up_r - HALO : up_r, 0:cols] = before[2 * layers]
    right = packs[0, 2 * groups]
    left = pltpu.roll(packs[1, 2 * groups], LANES - HALO, 1)
    edge = jnp.where(lane < LANES // 2, right, left)
    code_s[0:rows, cols:] = edge[0:rows]
    code_s[rows : rows + HALO, cols:] = edge[rows : rows + HALO]
    code_s[up_r - HALO : up_r, cols:] = edge[rows + HALO :]

    fr, fc = face.shape[1:]
    up_rows = (iota((up_r, fr), 0) // 2 == iota((up_r, fr), 1)).astype(jnp.float32)
    up_cols = (iota((fc, ext_c), 0) == iota((fc, ext_c), 1) // 2).astype(jnp.float32)
    for n in range(2):
        tall = jnp.dot(up_rows, face[n], precision=HIGHEST, preferred_element_type=jnp.float32)
        up_s[n] = jnp.dot(tall, up_cols, precision=HIGHEST, preferred_element_type=jnp.float32)
    gas_s[...] = jnp.zeros((up_r, ext_c), jnp.float32)
    film_s[...] = jnp.zeros((up_r, ext_c), jnp.float32)

    def pick_body(j, carry):
        shift = lax.rem(ext_c + 2 * DISP - 2 * j, ext_c)
        gas_w = pltpu.roll(up_s[0], shift, 1)
        film_w = pltpu.roll(up_s[1], shift, 1)
        for r in range(SPAN):
            down = (2 * DISP - 2 * r) % up_r
            hit = code_s[...] == (r * SPAN + j).astype(jnp.float32)
            gas_s[...] = jnp.where(hit, pltpu.roll(gas_w, down, 0) if down else gas_w, gas_s[...])
            film_s[...] = jnp.where(hit, pltpu.roll(film_w, down, 0) if down else film_w, film_s[...])
        return carry

    lax.fori_loop(0, SPAN, pick_body, 0)

    surf = a[0]
    flux_s[0:rows] = film_s[0:rows] * (gas_s[0:rows] - surf[0:rows])
    half = rows + HALO
    flux_s[rows:half] = film_s[rows:half] * (gas_s[rows:half] - surf[rows:half])
    tail = slice(up_r - HALO, up_r)
    flux_s[half:] = film_s[tail] * (gas_s[tail] - surf[half:])

    bufs = (a, b)
    for step in range(SUBSTEPS):
        src, dst = bufs[step % 2], bufs[(step + 1) % 2]
        last = step == SUBSTEPS - 1

        def body(z, carry, src=src, dst=dst, last=last):
            if last:
                full = src[z]
                c = full[0:rows]
                below = src[jnp.maximum(z - 1, 0), 0:rows, :]
                above = src[z + 1, 0:rows, :]
                coef = dd[z, 0:rows, :]
            else:
                full = c = src[z]
                below = src[jnp.maximum(z - 1, 0)]
                above = src[z + 1]
                coef = dd[z]
            n = c.shape[0]
            nearby = below + above + pltpu.roll(full, 1, 0)[0:n] + pltpu.roll(full, ext_r - 1, 0)[0:n]
            nearby = nearby + pltpu.roll(c, 1, 1) + pltpu.roll(c, ext_c - 1, 1)
            out = c + coef * (nearby - 6.0 * c)
            if last:
                s_out[z] = out[:, 0:cols]
            else:
                dst[z] = out
            return carry

        lax.fori_loop(0, layers, body, 0)
        if last:
            s_out[0] = s_out[0] + SOURCE_GAIN * flux_s[0:rows, 0:cols]
        else:
            dst[0] = dst[0] + SOURCE_GAIN * flux_s[...]

    hr, hc = rows // 2, cols // 2
    fold_r = 0.5 * (iota((hr, rows), 0) == iota((hr, rows), 1) // 2).astype(jnp.float32)
    fold_c = 0.5 * (iota((cols, hc), 0) // 2 == iota((cols, hc), 1)).astype(jnp.float32)
    short = jnp.dot(fold_r, s_out[0], precision=HIGHEST, preferred_element_type=jnp.float32)
    tile_out[...] = jnp.dot(short, fold_c, precision=HIGHEST, preferred_element_type=jnp.float32)


def shards(gas_temp, fuel_frac, velocity, wall_flags, solid_temp, diffusivity, gas_owner):
    nx, ny, nz = lax.axis_size("gx"), lax.axis_size("gy"), lax.axis_size("gz")
    gx, gy, gz = lax.axis_index("gx"), lax.axis_index("gy"), lax.axis_index("gz")
    assert ny == nz
    layers_g, rows_g, cols_g = gas_temp.shape
    layers, rows, cols = solid_temp.shape
    assert cols == 2 * cols_g and rows * ny == 2 * rows_g and 2 * layers_g <= LANES
    strip = rows // 2
    everywhere = ("gx", "gy", "gz")

    def rank(i, j, k):
        return (i * ny + j) * nz + k

    gas_face = gas_temp[0]
    film = FILM_COEF * wall_flags.astype(jnp.float32) * gas_face**0.7
    pair = jnp.stack([gas_face, film])
    after, before = exchange(pair[:, :8], pair[:, -8:], "gx")
    pair = jnp.concatenate([before, pair, after], axis=1)
    side = 32
    after, before = exchange(pair[:, :, :side], pair[:, :, -side:], "gy")
    ext_c = cols + LANES
    ext_half = ext_c // 2
    pair = jnp.concatenate([pair, after, before], axis=2)
    assert pair.shape[2] == ext_half
    pair = jnp.pad(pair, ((0, 0), (0, 0), (0, -ext_half % LANES)))

    all_cols = cols_g * ny
    all_rows = rows_g * nx
    p = (gx * ny + gy) * strip + iota((rows, cols), 0) // 2
    q = gz * cols_g + iota((rows, cols), 1) // 2
    down = (gas_owner // all_cols - p + DISP + all_rows) % all_rows
    along = (gas_owner % all_cols - q + DISP + all_cols) % all_cols
    code = (down * SPAN + along).astype(jnp.float32)

    last_g = cols_g // LANES - 1
    last_w = cols // LANES - 1
    groups = 2 * (layers // (LANES // HALO)) + 1

    def lane_tile(lead, index):
        shape = tuple(lead) + (LANES,)
        return pl.BlockSpec(shape, lambda i: (0,) * len(lead) + (index,))

    gas_lead, wall_lead = (layers_g, rows_g), (layers, rows)
    gas_edges, wall_edges = pl.pallas_call(
        pack_kernel,
        grid=(1,),
        out_shape=(
            jax.ShapeDtypeStruct((2, rows_g, LANES), jnp.float32),
            jax.ShapeDtypeStruct((2, groups, rows, LANES), jnp.float32),
        ),
        in_specs=[
            lane_tile(gas_lead, 0),
            lane_tile(gas_lead, last_g),
            lane_tile(gas_lead, 0),
            lane_tile(gas_lead, last_g),
            lane_tile(wall_lead, 0),
            lane_tile(wall_lead, last_w),
            lane_tile(wall_lead, 0),
            lane_tile(wall_lead, last_w),
            lane_tile((rows,), 0),
            lane_tile((rows,), last_w),
        ],
        compiler_params=pltpu.CompilerParams(vmem_limit_bytes=32 << 20),
        cost_estimate=pl.CostEstimate(flops=4_000_000, bytes_accessed=8 << 20, transcendentals=0),
        name="pack",
    )(gas_temp, gas_temp, fuel_frac, fuel_frac, solid_temp, solid_temp, diffusivity, diffusivity, code, code)

    y_high, y_low = exchange(gas_edges[0], gas_edges[1], "gy")
    x_high, x_low = exchange(
        jnp.stack([gas_temp[:, 0], fuel_frac[:, 0]]), jnp.stack([gas_temp[:, -1], fuel_frac[:, -1]]), "gx"
    )
    first = jnp.stack([gas_temp[0], fuel_frac[0]])
    final = jnp.stack([gas_temp[-1], fuel_frac[-1]])
    z_high, z_low = exchange(first, final, "gz")
    z_low = jnp.where(gz == 0, first, z_low)
    z_high = jnp.where(gz == nz - 1, final, z_high)

    line = ("gx", "gy")

    def edge_rows(cut):
        return jnp.concatenate([solid_temp[:, cut], diffusivity[:, cut], code[None, cut]], axis=0)

    rows_first, rows_last, y_low, y_high, pair = lax.optimization_barrier(
        (edge_rows(slice(0, HALO)), edge_rows(slice(rows - HALO, rows)), y_low, y_high, pair)
    )
    rows_after, rows_before = exchange(rows_first, rows_last, line)
    side_after, side_before = exchange(wall_edges[0], wall_edges[1], "gz")
    sides = jnp.stack([side_after, side_before])

    step_layers = 4
    block = (step_layers, rows_g, cols_g)
    temp_new, fuel_new = pl.pallas_call(
        functools.partial(gas_kernel, step_layers),
        grid=(layers_g // step_layers,),
        out_shape=(jax.ShapeDtypeStruct(gas_temp.shape, jnp.float32),) * 2,
        in_specs=[VMEM, VMEM, pl.BlockSpec((3,) + block, lambda i: (0, i, 0, 0))] + [VMEM] * 6,
        out_specs=(pl.BlockSpec(block, lambda i: (i, 0, 0)),) * 2,
        compiler_params=pltpu.CompilerParams(vmem_limit_bytes=32 << 20),
        cost_estimate=pl.CostEstimate(flops=60_000_000, bytes_accessed=24 << 20, transcendentals=1 << 19),
        name="gas",
    )(gas_temp, fuel_frac, velocity, x_low, x_high, y_low, y_high, z_low, z_high)

    sides, pair, temp_new = lax.optimization_barrier((sides, pair, temp_new))
    pad_rows = -(strip + 2 * REACH) % 8
    face = None
    for j in range(ny):
        top = 8 + j * strip
        band = jnp.concatenate(
            [
                pair[:, top : top + strip + REACH],
                pair[:, top - REACH : top],
                jnp.zeros((2, pad_rows, pair.shape[2]), jnp.float32),
            ],
            axis=1,
        )
        pairs = [(rank(i, k, 0), rank(i, j, k)) for i in range(nx) for k in range(ny)]
        got = lax.ppermute(band, everywhere, pairs)
        face = got if face is None else face + got

    corner_after, corner_before = exchange(sides[:, :, :HALO], sides[:, :, -HALO:], line)
    packs = jnp.concatenate([sides, corner_after, corner_before], axis=2)

    ext_r = rows + 2 * HALO
    up_r = rows + 4 * REACH
    ext = pltpu.VMEM((layers + 1, ext_r, ext_c), jnp.float32)
    up = pltpu.VMEM((up_r, ext_c), jnp.float32)
    solid_new, tile = pl.pallas_call(
        wall_kernel,
        out_shape=(
            jax.ShapeDtypeStruct(solid_temp.shape, jnp.float32),
            jax.ShapeDtypeStruct((strip, cols_g), jnp.float32),
        ),
        in_specs=[VMEM] * 7,
        out_specs=(VMEM, VMEM),
        scratch_shapes=[
            ext,
            ext,
            ext,
            up,
            up,
            up,
            pltpu.VMEM((2, up_r, ext_c), jnp.float32),
            pltpu.VMEM((ext_r, ext_c), jnp.float32),
        ],
        compiler_params=pltpu.CompilerParams(vmem_limit_bytes=58 << 20),
        cost_estimate=pl.CostEstimate(flops=120_000_000, bytes_accessed=40 << 20, transcendentals=0),
        name="wall",
    )(solid_temp, diffusivity, code, rows_after, rows_before, packs, face)

    bands = []
    for j in range(ny):
        pairs = [(rank(i, j, k), rank(i, k, 0)) for i in range(nx) for k in range(ny)]
        bands.append(lax.ppermute(tile, everywhere, pairs))
    wall_temp = jnp.concatenate(bands, axis=0)
    coupled = (wall_flags == 1) & (gz == 0)
    gap = jnp.where(coupled, 2.0 * (wall_temp - gas_face), 0.0)
    wall_term = TIME_STEP * (0.5 * velocity[0, 0] + DIFFUSE_TEMP) * gap
    temp_new = temp_new.at[0].add(wall_term)
    return (temp_new, fuel_new, solid_new)


def solution(mesh):
    placed = (
        P("gz", "gx", "gy"),
        P("gz", "gx", "gy"),
        P(None, "gz", "gx", "gy"),
        P("gx", "gy"),
        P(None, ("gx", "gy"), "gz"),
        P(None, ("gx", "gy"), "gz"),
        P(("gx", "gy"), "gz"),
    )
    return jax.shard_map(
        shards,
        mesh=mesh,
        in_specs=placed,
        out_specs=(P("gz", "gx", "gy"), P("gz", "gx", "gy"), P(None, ("gx", "gy"), "gz")),
        check_vma=False,
    )
```

profile of v0, /device:TPU:28, one launch (start us, length us, event | category | flops | bytes accessed | tf_op | source)
XLA Modules:
  0.0 173.9 jit_solution(17301475009134631803)
XLA Ops:
  0.7 1.0 fusion.8.c_lo.c_hi.code
  1.7 2.2 %copy-done = f32[64,32,512]{2,1,0:T(8,128)S(1)} copy-done((f32[64,32,512]{2,1,0:T(8,128)S(1)}, f32[64,32,512]{2,1,0:T(8,128)}, u32[]{:S(2)}) %copy-start) | copy-done | bytes 4194328
  3.9 2.2 %copy-done.1 = f32[64,32,512]{2,1,0:T(8,128)S(1)} copy-done((f32[64,32,512]{2,1,0:T(8,128)S(1)}, f32[64,32,512]{2,1,0:T(8,128)}, u32[]{:S(2)}) %copy-start.1) | copy-done | bytes 4194328
  6.0 1.6 copy-done.2
  7.6 1.6 copy-done.4
  9.2 9.5 %pack.1 = (f32[2,64,128]{2,1,0:T(8,128)S(1)}, f32[2,5,32,128]{3,2,1,0:T(8,128)S(1)}) custom-call(f32[32,64,256]{2,1,0:T(8,128)S(1)} %copy-done.2, f32[32,64,256]{2,1,0:T(8,128)S(1)} %copy-done.2, f32[32,64,256]{2,1,0:T(8,128)S(1)} %copy-done.4, f32[32,64,256]{2,1,0:T(8,128)S(1)} %copy-done.4, f32[64,32,512]{2,1,0:T(8,128)S(1)} %copy-done, ...), custom_call_target="tpu_custom_call" | custom-call | flops 4000000 | bytes 8388608 | tf_op jit(solution)/shard_map/pack/pallas_call | solution.py:277
  18.7 0.6 slice_bitcast_fusion.2
  19.3 0.4 collective-permute-start.3
  19.8 3.4 %collective-permute-start.2 = (f32[64,128]{1,0:T(8,128)}, f32[64,128]{1,0:T(8,128)S(1)}, u32[]{:S(2)}, u32[]{:S(2)}) collective-permute-start(f32[64,128]{1,0:T(8,128)} %get-tuple-element.74), channel_id=1, source_target_pairs={{0,4},{4,8},{8,12},{12,0},{1,5},{5,9},{9,13},{13,1},{2,6},{6,10},{... | collective-permute-start | bytes 98312 | tf_op jit(solution)/shard_map/ppermute | solution.py:42
  23.2 0.7 slice_bitcast_fusion.1
  23.8 0.4 collective-permute-start
  24.2 0.6 fusion.27
  24.8 0.1 fusion.19
  24.9 0.6 fusion.21
  25.5 0.5 collective-permute-start.4
  26.0 1.5 collective-permute-start.5
  27.6 0.5 fusion.25
  28.2 0.7 pad_maximum_fusion.5
  28.8 0.6 pad_maximum_fusion.8
  29.5 0.2 pad_maximum_fusion.1
  29.7 1.2 pad_maximum_fusion
  30.9 0.6 pad_maximum_fusion.7
  31.6 0.1 pad.22.clone
  31.6 0.7 collective-permute-start.11
  32.3 0.7 pad_maximum_fusion.4
  33.1 0.1 fusion.34
  33.1 0.1 collective-permute-start.6
  33.2 1.9 %collective-permute-done.11 = f32[2,64,256]{2,1,0:T(8,128)S(1)} collective-permute-done((f32[2,64,256]{2,1,0:T(8,128)}, f32[2,64,256]{2,1,0:T(8,128)S(1)}, u32[]{:S(2)}, u32[]{:S(2)}) %collective-permute-start.11) | collective-permute-done | bytes 131104 | tf_op jit(solution)/shard_map/ppermute | solution.py:42
  35.1 1.9 %collective-permute-start.7 = (f32[2,80,32]{2,1,0:T(8,128)S(1)}, f32[2,80,32]{2,1,0:T(8,128)S(1)}, u32[]{:S(2)}, u32[]{:S(2)}) collective-permute-start(f32[2,80,32]{2,1,0:T(8,128)S(1)} %get-tuple-element.66), channel_id=1, source_target_pairs={{0,4},{4,8},{8,12},{12,0},{1,5},{5,9},{9,13},{13,1},{2,6},{6,10},{... | collective-permute-start | bytes 61448 | tf_op jit(solution)/shard_map/ppermute | solution.py:42
  37.0 0.9 broadcast_select_fusion
  37.9 2.2 %collective-permute-done.6 = f32[2,80,32]{2,1,0:T(8,128)S(1)} collective-permute-done((f32[2,80,32]{2,1,0:T(8,128)S(1)}, f32[2,80,32]{2,1,0:T(8,128)S(1)}, u32[]{:S(2)}, u32[]{:S(2)}) %collective-permute-start.6) | collective-permute-done | bytes 20512 | tf_op jit(solution)/shard_map/ppermute | solution.py:42
  40.1 0.9 collective-permute-done.7
  41.0 0.1 collective-permute-start.10
  41.1 0.8 select_maximum_fusion
  42.0 0.6 collective-permute-start.8
  42.5 1.5 collective-permute-start.9
  44.1 0.1 collective-permute-done.1
  44.2 4.6 %collective-permute-start.13 = (f32[129,4,512]{2,1,0:T(4,128)S(1)}, f32[129,4,512]{2,1,0:T(4,128)S(1)}, u32[]{:S(2)}, u32[]{:S(2)}) collective-permute-start(f32[129,4,512]{2,1,0:T(4,128)S(1)} %pad_maximum_fusion.1), channel_id=1, source_target_pairs={{0,4},{4,8},{8,12},{12,16},{16,20},{20,24},{24,28},{28,0},{1,5},{5... | collective-permute-start | bytes 3170312 | tf_op jit(solution)/shard_map/ppermute | solution.py:42
  48.8 0.9 pad_maximum_fusion.3
  49.8 0.0 copy-start.6
  49.8 2.8 %copy-done.6 = f32[3,32,64,256]{3,2,1,0:T(8,128)S(1)} copy-done((f32[3,32,64,256]{3,2,1,0:T(8,128)S(1)}, f32[3,32,64,256]{3,2,1,0:T(8,128)}, u32[]{:S(2)}) %copy-start.6) | copy-done | bytes 6291480
  52.6 6.7 %gas.1 = (f32[32,64,256]{2,1,0:T(8,128)}, f32[32,64,256]{2,1,0:T(8,128)}) custom-call(f32[32,64,256]{2,1,0:T(8,128)S(1)} %copy-done.3, f32[32,64,256]{2,1,0:T(8,128)S(1)} %copy-done.5, f32[3,32,64,256]{3,2,1,0:T(8,128)S(1)} %copy-done.6, f32[2,32,256]{2,1,0:T(8,128)S(1)} %collective-permute-done.8.x_low, f32[2,32,256]{2,1,0:T(8,128)S(1)} %collective-permute-done.9.x_high, ...), custom_call_target="tpu_custom_call" | custom-call | flops 60000000 | bytes 25165824 | tf_op jit(solution)/shard_map/gas/pallas_call | solution.py:325
  59.3 0.1 maximum_maximum_fusion.1
  59.4 1.5 collective-permute-start.17
  60.9 0.9 collective-permute-start.14
  61.8 3.9 %collective-permute-start.15 = (f32[2,5,4,128]{3,2,1,0:T(4,128)S(1)}, f32[2,5,4,128]{3,2,1,0:T(4,128)S(1)}, u32[]{:S(2)}, u32[]{:S(2)}) collective-permute-start(f32[2,5,4,128]{3,2,1,0:T(4,128)S(1)} %get-tuple-element.64), channel_id=1, source_target_pairs={{0,4},{4,8},{8,12},{12,16},{16,20},{20,24},{24,28},{28,0},{1,5},{5... | collective-permute-start | bytes 61448 | tf_op jit(solution)/shard_map/ppermute | solution.py:42
  65.7 31.5 %collective-permute-done.14 = f32[2,5,4,128]{3,2,1,0:T(4,128)S(1)} collective-permute-done((f32[2,5,4,128]{3,2,1,0:T(4,128)S(1)}, f32[2,5,4,128]{3,2,1,0:T(4,128)S(1)}, u32[]{:S(2)}, u32[]{:S(2)}) %collective-permute-start.14) | collective-permute-done | bytes 20512 | tf_op jit(solution)/shard_map/ppermute | solution.py:42
  97.1 1.3 collective-permute-start.18
  98.5 1.9 %collective-permute-start.19 = (f32[2,32,384]{2,1,0:T(8,128)S(1)}, f32[2,32,384]{2,1,0:T(8,128)S(1)}, u32[]{:S(2)}, u32[]{:S(2)}) collective-permute-start(f32[2,32,384]{2,1,0:T(8,128)S(1)} %get-tuple-element.79), channel_id=1, source_target_pairs={{0,12},{4,13},{8,14},{12,15},{16,28},{20,29},{24,30},{28,31}} | collective-permute-start | bytes 294920 | tf_op jit(solution)/shard_map/ppermute | solution.py:350
  100.4 1.3 collective-permute-start.16
  101.7 0.7 pad_maximum_fusion.2.packs
  102.4 4.3 %collective-permute-done.19 = f32[2,32,384]{2,1,0:T(8,128)S(1)} collective-permute-done((f32[2,32,384]{2,1,0:T(8,128)S(1)}, f32[2,32,384]{2,1,0:T(8,128)S(1)}, u32[]{:S(2)}, u32[]{:S(2)}) %collective-permute-start.19) | collective-permute-done | bytes 98336 | tf_op jit(solution)/shard_map/ppermute | solution.py:350
  106.8 0.7 add_add_fusion.face
  107.4 1.0 copy-done.8
  108.4 1.0 copy-done.9
  109.4 50.5 %wall.1 = (f32[64,32,512]{2,1,0:T(8,128)}, f32[16,256]{1,0:T(8,128)}) custom-call(f32[64,32,512]{2,1,0:T(8,128)} %s.1, f32[64,32,512]{2,1,0:T(8,128)} %d.1, f32[32,512]{1,0:T(8,128)} %copy-done.7, f32[129,4,512]{2,1,0:T(4,128)} %copy-done.8, f32[129,4,512]{2,1,0:T(4,128)} %copy-done.9, f32[2,5,40,128]{3,2,1,0:T(8,128)} %pad_maximum_fusion.2.packs, ...), custom_call_target="tpu_custom_call" | custom-call | flops 120000000 | bytes 41943040 | tf_op jit(solution)/shard_map/wall/pallas_call | solution.py:360
  159.9 1.9 %collective-permute-start.23 = (f32[16,256]{1,0:T(8,128)}, f32[16,256]{1,0:T(8,128)S(1)}, u32[]{:S(2)}, u32[]{:S(2)}) collective-permute-start(f32[16,256]{1,0:T(8,128)} %get-tuple-element.40), channel_id=1, source_target_pairs={{12,0},{13,4},{14,8},{15,12},{28,16},{29,20},{30,24},{31,28}} | collective-permute-start | bytes 49160 | tf_op jit(solution)/shard_map/ppermute | solution.py:386
  161.8 1.3 collective-permute-start.22
  163.1 1.3 collective-permute-start.21
  164.4 1.3 collective-permute-start.20
  165.7 2.3 %collective-permute-done.22 = f32[16,256]{1,0:T(8,128)S(1)} collective-permute-done((f32[16,256]{1,0:T(8,128)}, f32[16,256]{1,0:T(8,128)S(1)}, u32[]{:S(2)}, u32[]{:S(2)}) %collective-permute-start.22) | collective-permute-done | bytes 16416 | tf_op jit(solution)/shard_map/ppermute | solution.py:386
  168.0 2.2 %collective-permute-done.21 = f32[16,256]{1,0:T(8,128)S(1)} collective-permute-done((f32[16,256]{1,0:T(8,128)}, f32[16,256]{1,0:T(8,128)S(1)}, u32[]{:S(2)}, u32[]{:S(2)}) %collective-permute-start.21) | collective-permute-done | bytes 16416 | tf_op jit(solution)/shard_map/ppermute | solution.py:386
  170.2 2.2 %collective-permute-done.20 = f32[16,256]{1,0:T(8,128)S(1)} collective-permute-done((f32[16,256]{1,0:T(8,128)}, f32[16,256]{1,0:T(8,128)S(1)}, u32[]{:S(2)}, u32[]{:S(2)}) %collective-permute-start.20) | collective-permute-done | bytes 16416 | tf_op jit(solution)/shard_map/ppermute | solution.py:386
  172.4 1.5 fusion.17
  (45 shorter events, 0.3 us)
Async XLA Ops:
  1.7 2.2 %copy-start = (f32[64,32,512]{2,1,0:T(8,128)S(1)}, f32[64,32,512]{2,1,0:T(8,128)}, u32[]{:S(2)}) copy-start(f32[64,32,512]{2,1,0:T(8,128)} %s.1) | copy-start | bytes 12582916
  3.9 2.2 %copy-start.1 = (f32[64,32,512]{2,1,0:T(8,128)S(1)}, f32[64,32,512]{2,1,0:T(8,128)}, u32[]{:S(2)}) copy-start(f32[64,32,512]{2,1,0:T(8,128)} %d.1) | copy-start | bytes 12582916
  6.0 1.6 copy-start.2
  7.6 1.6 copy-start.4
  9.2 18.3 %copy-start.7 = (f32[32,512]{1,0:T(8,128)}, f32[32,512]{1,0:T(8,128)S(1)}, u32[]{:S(2)}) copy-start(f32[32,512]{1,0:T(8,128)S(1)} %fusion.8.c_lo.c_hi.code) | copy-start | bytes 196612
  9.2 15.6 %copy-start.10 = (s32[64,256]{1,0:T(8,128)S(1)}, s32[64,256]{1,0:T(8,128)}, u32[]{:S(2)}) copy-start(s32[64,256]{1,0:T(8,128)} %param.12) | copy-start | bytes 196612
  19.3 22.6 %collective-permute-start.3 = (f32[64,128]{1,0:T(8,128)}, f32[64,128]{1,0:T(8,128)S(1)}, u32[]{:S(2)}, u32[]{:S(2)}) collective-permute-start(f32[64,128]{1,0:T(8,128)} %get-tuple-element.73), channel_id=1, source_target_pairs={{4,0},{8,4},{12,8},{0,12},{5,1},{9,5},{13,9},{1,13},{6,2},{10,6},{... | collective-permute-start | bytes 98312 | tf_op jit(solution)/shard_map/ppermute | solution.py:42
  19.8 22.8 %collective-permute-start.2 = (f32[64,128]{1,0:T(8,128)}, f32[64,128]{1,0:T(8,128)S(1)}, u32[]{:S(2)}, u32[]{:S(2)}) collective-permute-start(f32[64,128]{1,0:T(8,128)} %get-tuple-element.74), channel_id=1, source_target_pairs={{0,4},{4,8},{8,12},{12,0},{1,5},{5,9},{9,13},{13,1},{2,6},{6,10},{... | collective-permute-start | bytes 98312 | tf_op jit(solution)/shard_map/ppermute | solution.py:42
  23.8 20.2 %collective-permute-start = (f32[5,32,128]{2,1,0:T(8,128)}, f32[5,32,128]{2,1,0:T(8,128)}, u32[]{:S(2)}, u32[]{:S(2)}) collective-permute-start(f32[5,32,128]{2,1,0:T(8,128)} %get-tuple-element.67), channel_id=1, source_target_pairs={{1,0},{2,1},{3,2},{0,3},{5,4},{6,5},{7,6},{4,7},{9,8},{10,9},{11,1... | collective-permute-start | bytes 245768 | tf_op jit(solution)/shard_map/ppermute | solution.py:42
  25.5 6.1 %collective-permute-start.4 = (f32[2,8,256]{2,1,0:T(8,128)}, f32[2,8,256]{2,1,0:T(8,128)}, u32[]{:S(2)}, u32[]{:S(2)}) collective-permute-start(f32[2,8,256]{2,1,0:T(8,128)} %get-tuple-element.71), channel_id=1, source_target_pairs={{0,16},{16,0},{1,17},{17,1},{2,18},{18,2},{3,19},{19,3},{4,20},{20... | collective-permute-start | bytes 49160 | tf_op jit(solution)/shard_map/ppermute | solution.py:42
  26.0 6.3 %collective-permute-start.5 = (f32[2,8,256]{2,1,0:T(8,128)}, f32[2,8,256]{2,1,0:T(8,128)}, u32[]{:S(2)}, u32[]{:S(2)}) collective-permute-start(f32[2,8,256]{2,1,0:T(8,128)} %get-tuple-element.72), channel_id=1, source_target_pairs={{16,0},{0,16},{17,1},{1,17},{18,2},{2,18},{19,3},{3,19},{20,4},{4,... | collective-permute-start | bytes 49160 | tf_op jit(solution)/shard_map/ppermute | solution.py:42
  29.7 20.0 %copy-start.3 = (f32[32,64,256]{2,1,0:T(8,128)S(1)}, f32[32,64,256]{2,1,0:T(8,128)}, u32[]{:S(2)}) copy-start(f32[32,64,256]{2,1,0:T(8,128)} %temp.1) | copy-start | bytes 6291460
  31.5 18.2 %copy-start.5 = (f32[32,64,256]{2,1,0:T(8,128)S(1)}, f32[32,64,256]{2,1,0:T(8,128)}, u32[]{:S(2)}) copy-start(f32[32,64,256]{2,1,0:T(8,128)} %fuel.1) | copy-start | bytes 6291460
  31.6 3.5 %collective-permute-start.11 = (f32[2,64,256]{2,1,0:T(8,128)}, f32[2,64,256]{2,1,0:T(8,128)S(1)}, u32[]{:S(2)}, u32[]{:S(2)}) collective-permute-start(f32[2,64,256]{2,1,0:T(8,128)} %pad_maximum_fusion.5), channel_id=1, source_target_pairs={{1,0},{2,1},{3,2},{0,3},{5,4},{6,5},{7,6},{4,7},{9,8},{10,9},{11,1... | collective-permute-start | bytes 393224 | tf_op jit(solution)/shard_map/ppermute | solution.py:42
  33.1 7.0 %collective-permute-start.6 = (f32[2,80,32]{2,1,0:T(8,128)S(1)}, f32[2,80,32]{2,1,0:T(8,128)S(1)}, u32[]{:S(2)}, u32[]{:S(2)}) collective-permute-start(f32[2,80,32]{2,1,0:T(8,128)S(1)} %get-tuple-element.65), channel_id=1, source_target_pairs={{4,0},{8,4},{12,8},{0,12},{5,1},{9,5},{13,9},{1,13},{6,2},{10,6},{... | collective-permute-start | bytes 61448 | tf_op jit(solution)/shard_map/ppermute | solution.py:42
  35.1 5.9 %collective-permute-start.7 = (f32[2,80,32]{2,1,0:T(8,128)S(1)}, f32[2,80,32]{2,1,0:T(8,128)S(1)}, u32[]{:S(2)}, u32[]{:S(2)}) collective-permute-start(f32[2,80,32]{2,1,0:T(8,128)S(1)} %get-tuple-element.66), channel_id=1, source_target_pairs={{0,4},{4,8},{8,12},{12,0},{1,5},{5,9},{9,13},{13,1},{2,6},{6,10},{... | collective-permute-start | bytes 61448 | tf_op jit(solution)/shard_map/ppermute | solution.py:42
  40.1 4.1 %collective-permute-start.1 = (f32[5,32,128]{2,1,0:T(8,128)}, f32[5,32,128]{2,1,0:T(8,128)S(1)}, u32[]{:S(2)}, u32[]{:S(2)}) collective-permute-start(f32[5,32,128]{2,1,0:T(8,128)} %get-tuple-element.68), channel_id=1, source_target_pairs={{0,1},{1,2},{2,3},{3,0},{4,5},{5,6},{6,7},{7,4},{8,9},{9,10},{10,1... | collective-permute-start | bytes 245768 | tf_op jit(solution)/shard_map/ppermute | solution.py:42
  41.0 8.7 %collective-permute-start.10 = (f32[2,64,256]{2,1,0:T(8,128)S(1)}, f32[2,64,256]{2,1,0:T(8,128)S(1)}, u32[]{:S(2)}, u32[]{:S(2)}) collective-permute-start(f32[2,64,256]{2,1,0:T(8,128)S(1)} %get-tuple-element.70), channel_id=1, source_target_pairs={{0,1},{1,2},{2,3},{3,0},{4,5},{5,6},{6,7},{7,4},{8,9},{9,10},{10,1... | collective-permute-start | bytes 393224 | tf_op jit(solution)/shard_map/ppermute | solution.py:42
  42.0 7.8 %collective-permute-start.8 = (f32[2,32,256]{2,1,0:T(8,128)}, f32[2,32,256]{2,1,0:T(8,128)S(1)}, u32[]{:S(2)}, u32[]{:S(2)}) collective-permute-start(f32[2,32,256]{2,1,0:T(8,128)} %pad_maximum_fusion.7), channel_id=1, source_target_pairs={{0,16},{16,0},{1,17},{17,1},{2,18},{18,2},{3,19},{19,3},{4,20},{20... | collective-permute-start | bytes 196616 | tf_op jit(solution)/shard_map/ppermute | solution.py:42
  42.5 7.2 %collective-permute-start.9 = (f32[2,32,256]{2,1,0:T(8,128)}, f32[2,32,256]{2,1,0:T(8,128)S(1)}, u32[]{:S(2)}, u32[]{:S(2)}) collective-permute-start(f32[2,32,256]{2,1,0:T(8,128)} %pad_maximum_fusion.8), channel_id=1, source_target_pairs={{16,0},{0,16},{17,1},{1,17},{18,2},{2,18},{19,3},{3,19},{20,4},{4,... | collective-permute-start | bytes 196616 | tf_op jit(solution)/shard_map/ppermute | solution.py:42
  44.1 63.4 %collective-permute-start.12 = (f32[129,4,512]{2,1,0:T(4,128)}, f32[129,4,512]{2,1,0:T(4,128)S(1)}, u32[]{:S(2)}, u32[]{:S(2)}) collective-permute-start(f32[129,4,512]{2,1,0:T(4,128)} %pad_maximum_fusion), channel_id=1, source_target_pairs={{4,0},{8,4},{12,8},{16,12},{20,16},{24,20},{28,24},{0,28},{5,1},{9... | collective-permute-start | bytes 3170312 | tf_op jit(solution)/shard_map/ppermute | solution.py:42
  44.2 63.3 %collective-permute-start.13 = (f32[129,4,512]{2,1,0:T(4,128)S(1)}, f32[129,4,512]{2,1,0:T(4,128)S(1)}, u32[]{:S(2)}, u32[]{:S(2)}) collective-permute-start(f32[129,4,512]{2,1,0:T(4,128)S(1)} %pad_maximum_fusion.1), channel_id=1, source_target_pairs={{0,4},{4,8},{8,12},{12,16},{16,20},{20,24},{24,28},{28,0},{1,5},{5... | collective-permute-start | bytes 3170312 | tf_op jit(solution)/shard_map/ppermute | solution.py:42
  49.8 2.8 %copy-start.6 = (f32[3,32,64,256]{3,2,1,0:T(8,128)S(1)}, f32[3,32,64,256]{3,2,1,0:T(8,128)}, u32[]{:S(2)}) copy-start(f32[3,32,64,256]{3,2,1,0:T(8,128)} %vel.1) | copy-start | bytes 18874372
  59.4 41.0 %collective-permute-start.17 = (f32[2,32,384]{2,1,0:T(8,128)S(1)}, f32[2,32,384]{2,1,0:T(8,128)S(1)}, u32[]{:S(2)}, u32[]{:S(2)}) collective-permute-start(f32[2,32,384]{2,1,0:T(8,128)S(1)} %get-tuple-element.77), channel_id=1, source_target_pairs={{0,4},{4,5},{8,6},{12,7},{16,20},{20,21},{24,22},{28,23}} | collective-permute-start | bytes 294920 | tf_op jit(solution)/shard_map/ppermute | solution.py:350
  60.9 36.3 %collective-permute-start.14 = (f32[2,5,4,128]{3,2,1,0:T(4,128)S(1)}, f32[2,5,4,128]{3,2,1,0:T(4,128)S(1)}, u32[]{:S(2)}, u32[]{:S(2)}) collective-permute-start(f32[2,5,4,128]{3,2,1,0:T(4,128)S(1)} %get-tuple-element.63), channel_id=1, source_target_pairs={{4,0},{8,4},{12,8},{16,12},{20,16},{24,20},{28,24},{0,28},{5,1},{9... | collective-permute-start | bytes 61448 | tf_op jit(solution)/shard_map/ppermute | solution.py:42
  61.8 36.7 %collective-permute-start.15 = (f32[2,5,4,128]{3,2,1,0:T(4,128)S(1)}, f32[2,5,4,128]{3,2,1,0:T(4,128)S(1)}, u32[]{:S(2)}, u32[]{:S(2)}) collective-permute-start(f32[2,5,4,128]{3,2,1,0:T(4,128)S(1)} %get-tuple-element.64), channel_id=1, source_target_pairs={{0,4},{4,8},{8,12},{12,16},{16,20},{20,24},{24,28},{28,0},{1,5},{5... | collective-permute-start | bytes 61448 | tf_op jit(solution)/shard_map/ppermute | solution.py:42
  97.1 5.3 %collective-permute-start.18 = (f32[2,32,384]{2,1,0:T(8,128)S(1)}, f32[2,32,384]{2,1,0:T(8,128)S(1)}, u32[]{:S(2)}, u32[]{:S(2)}) collective-permute-start(f32[2,32,384]{2,1,0:T(8,128)S(1)} %get-tuple-element.78), channel_id=1, source_target_pairs={{0,8},{4,9},{8,10},{12,11},{16,24},{20,25},{24,26},{28,27}} | collective-permute-start | bytes 294920 | tf_op jit(solution)/shard_map/ppermute | solution.py:350
  98.5 8.3 %collective-permute-start.19 = (f32[2,32,384]{2,1,0:T(8,128)S(1)}, f32[2,32,384]{2,1,0:T(8,128)S(1)}, u32[]{:S(2)}, u32[]{:S(2)}) collective-permute-start(f32[2,32,384]{2,1,0:T(8,128)S(1)} %get-tuple-element.79), channel_id=1, source_target_pairs={{0,12},{4,13},{8,14},{12,15},{16,28},{20,29},{24,30},{28,31}} | collective-permute-start | bytes 294920 | tf_op jit(solution)/shard_map/ppermute | solution.py:350
  100.4 6.4 %collective-permute-start.16 = (f32[2,32,384]{2,1,0:T(8,128)S(1)}, f32[2,32,384]{2,1,0:T(8,128)S(1)}, u32[]{:S(2)}, u32[]{:S(2)}) collective-permute-start(f32[2,32,384]{2,1,0:T(8,128)S(1)} %get-tuple-element.80), channel_id=1, source_target_pairs={{0,0},{4,1},{8,2},{12,3},{16,16},{20,17},{24,18},{28,19}} | collective-permute-start | bytes 294920 | tf_op jit(solution)/shard_map/ppermute | solution.py:350
  107.4 1.0 copy-start.8
  108.4 1.0 copy-start.9
  159.9 5.8 %collective-permute-start.23 = (f32[16,256]{1,0:T(8,128)}, f32[16,256]{1,0:T(8,128)S(1)}, u32[]{:S(2)}, u32[]{:S(2)}) collective-permute-start(f32[16,256]{1,0:T(8,128)} %get-tuple-element.40), channel_id=1, source_target_pairs={{12,0},{13,4},{14,8},{15,12},{28,16},{29,20},{30,24},{31,28}} | collective-permute-start | bytes 49160 | tf_op jit(solution)/shard_map/ppermute | solution.py:386
  161.8 6.2 %collective-permute-start.22 = (f32[16,256]{1,0:T(8,128)}, f32[16,256]{1,0:T(8,128)S(1)}, u32[]{:S(2)}, u32[]{:S(2)}) collective-permute-start(f32[16,256]{1,0:T(8,128)} %get-tuple-element.40), channel_id=1, source_target_pairs={{8,0},{9,4},{10,8},{11,12},{24,16},{25,20},{26,24},{27,28}} | collective-permute-start | bytes 49160 | tf_op jit(solution)/shard_map/ppermute | solution.py:386
  163.1 7.1 %collective-permute-start.21 = (f32[16,256]{1,0:T(8,128)}, f32[16,256]{1,0:T(8,128)S(1)}, u32[]{:S(2)}, u32[]{:S(2)}) collective-permute-start(f32[16,256]{1,0:T(8,128)} %get-tuple-element.40), channel_id=1, source_target_pairs={{4,0},{5,4},{6,8},{7,12},{20,16},{21,20},{22,24},{23,28}} | collective-permute-start | bytes 49160 | tf_op jit(solution)/shard_map/ppermute | solution.py:386
  164.4 8.0 %collective-permute-start.20 = (f32[16,256]{1,0:T(8,128)}, f32[16,256]{1,0:T(8,128)S(1)}, u32[]{:S(2)}, u32[]{:S(2)}) collective-permute-start(f32[16,256]{1,0:T(8,128)} %get-tuple-element.40), channel_id=1, source_target_pairs={{0,0},{1,4},{2,8},{3,12},{16,16},{17,20},{18,24},{19,28}} | collective-permute-start | bytes 49160 | tf_op jit(solution)/shard_map/ppermute | solution.py:386
where the time goes:
time: 175 us; the launch traced here: 174 us
  Pallas kernels  66.6 us (38%)
  waiting for transfers between devices  47.7 us (27%)
  starting transfers between devices  32.1 us (18%)
  local copies, waits for them, and re-layouts  15.1 us (9%)
  other arithmetic  11.4 us (7%)
    pallas_call x1, Pallas kernels, shards(): pl.pallas_call(wall_kernel, out_shape=(jax.ShapeDtypeStruct(solid_temp.sh...  50.5 us
    ppermute x8, waiting for transfers between devices, exchange(): lax.ppermute(first, axis, backward)  35.7 us
    ppermute x8, starting transfers between devices, exchange(): lax.ppermute(last, axis, forward)  14.9 us
    unnamed x22, local copies, waits for them, and re-layouts  12.3 us
    pallas_call x1, Pallas kernels, shards(): pl.pallas_call(pack_kernel, grid=(1,), out_shape=(jax.ShapeDtypeStruct((2...  9.46 us
    pallas_call x1, Pallas kernels, shards(): pl.pallas_call(functools.partial(gas_kernel, step_layers), grid=(layers_g...  6.68 us
    ppermute x4, waiting for transfers between devices, shards(): bands.append(lax.ppermute(tile, everywhere, pairs))  6.66 us
    ppermute x4, starting transfers between devices, shards(): got = lax.ppermute(band, everywhere, pairs)  5.96 us
  transfers between devices with their start and end apart: 24, of which 9 were waited for; matrix products, arithmetic and copies ran while one was open for 6% of the time, Pallas kernels for 4%

commit v1 on v0

v1 whole, which is shorter than its diff:
```python
import functools

import jax
import jax.numpy as jnp
from jax import lax
from jax.experimental import pallas as pl
from jax.experimental.pallas import tpu as pltpu
from jax.sharding import PartitionSpec as P

SUBSTEPS = 4
DISP = 4

FILM_COEF = 0.15
SOURCE_GAIN = 0.25
COOLANT = 1.0
DIFFUSE_TEMP = 0.2
DIFFUSE_FUEL = 0.15
TIME_STEP = 0.2
RATE_CONST = 1.0
ACTIVATION = 4.0
HEAT_RELEASE = 3.0

LANES = 128
SUB = 8
CHUNK = 8
GROUP = LANES // CHUNK
HALO = SUBSTEPS
SPAN = 2 * DISP + 1
MESH = pl.DeviceIdType.MESH
ANY = pl.BlockSpec(memory_space=pl.ANY)


def iota(shape, dim):
    return lax.broadcasted_iota(jnp.int32, shape, dim)


def lanes_of(x, idx):
    return jnp.take_along_axis(x, idx, axis=1, mode="promise_in_bounds")


def mega_kernel(
    mesh_shape,
    temp_in,
    fuel_in,
    vel_in,
    flags_in,
    solid_in,
    diff_in,
    owner_in,
    temp_out,
    fuel_out,
    solid_out,
    G,
    V,
    FL,
    A,
    B,
    D,
    TO,
    FO,
    OW,
    E,
    EN,
    CO,
    CN,
    MS,
    MR,
    ZS,
    ZR,
    XS,
    XR,
    YS,
    YR,
    GS,
    GB,
    DW,
    F,
    WS,
    WR,
    load_s,
    load_d,
    load_g,
    load_m,
    out_sem,
    row_send,
    row_recv,
    zone_send,
    zone_recv,
    edge_send,
    edge_recv,
    code_send,
    code_recv,
    y_send,
    y_recv,
    x_send,
    x_recv,
    z_send,
    z_recv,
    face_send,
    face_recv,
    wt_send,
    wt_recv,
):
    nx, ny, nz = mesh_shape
    gx, gy, gz = lax.axis_index("gx"), lax.axis_index("gy"), lax.axis_index("gz")
    layers_g, rows_g, cols_g = temp_in.shape
    layers, rows, cols = solid_in.shape
    chunks = layers // CHUNK
    wt = cols // LANES
    gt = cols_g // LANES
    units = wt * CHUNK
    strip = rows // 2
    top = SUB
    rtiles = rows // SUB
    gtiles = rows_g // SUB
    steps = SUBSTEPS * chunks
    lane = iota((SUB, LANES), 1)

    def dev(x, y, z):
        return (x, y, z)

    def ring(i, n, by):
        return lax.rem(i + n + by, n)

    line = gx * ny + gy
    line_next, line_prev = ring(line, nx * ny, 1), ring(line, nx * ny, -1)
    row_dev = (
        dev(lax.div(line_next, ny), lax.rem(line_next, ny), gz),
        dev(lax.div(line_prev, ny), lax.rem(line_prev, ny), gz),
    )
    col_dev = (dev(gx, gy, ring(gz, nz, 1)), dev(gx, gy, ring(gz, nz, -1)))
    y_dev = (dev(gx, ring(gy, ny, 1), gz), dev(gx, ring(gy, ny, -1), gz))
    x_dev = (dev(ring(gx, nx, 1), gy, gz), dev(ring(gx, nx, -1), gy, gz))

    def remote(src, dst, ssem, rsem, to):
        return pltpu.make_async_remote_copy(
            src_ref=src, dst_ref=dst, send_sem=ssem, recv_sem=rsem, device_id=to, device_id_type=MESH
        )

    def load_gas(f, src, k):
        return pltpu.make_async_copy(
            src.at[:, :, pl.ds(k * LANES, LANES)],
            G.at[f, pl.ds(1, layers_g), k, pl.ds(top, rows_g), :],
            load_g.at[f, k],
        )

    def load_wall(src, c, k):
        if src is solid_in:
            dst = A.at[c, pl.ds(k * CHUNK, CHUNK), pl.ds(top, rows), :]
            sem = load_s.at[c, k]
        else:
            dst = D.at[c, pl.ds(k * CHUNK, CHUNK), :, :]
            sem = load_d.at[c, k]
        return pltpu.make_async_copy(src.at[pl.ds(c * CHUNK, CHUNK), :, pl.ds(k * LANES, LANES)], dst, sem)

    load_flags = pltpu.make_async_copy(flags_in, FL, load_m.at[0])
    load_owner = pltpu.make_async_copy(owner_in, OW, load_m.at[1])
    load_vel = pltpu.make_async_copy(vel_in, V, load_m.at[2])

    def store_wall(c, k):
        return pltpu.make_async_copy(
            A.at[c, pl.ds(k * CHUNK, CHUNK), pl.ds(top, rows), :],
            solid_out.at[pl.ds(c * CHUNK, CHUNK), :, pl.ds(k * LANES, LANES)],
            out_sem.at[2, c, k],
        )

    def store_gas(f, z):
        src, dst = ((TO, temp_out), (FO, fuel_out))[f]
        return pltpu.make_async_copy(src.at[z], dst.at[z], out_sem.at[f, lax.div(z, wt), lax.rem(z, wt)])

    def row_copy(t, c, way):
        count = pl.ds(0, units + 1)
        return remote(
            MS.at[way, t, c, count, :],
            MR.at[way, t, c, count, :],
            row_send.at[way, t, c],
            row_recv.at[way, t, c],
            row_dev[way],
        )

    def first_copy(c, way):
        count = pl.ds(0, units)
        return remote(
            MS.at[way, 0, c, count, :],
            MR.at[way, 0, c, count, :],
            row_send.at[way, 0, c],
            row_recv.at[way, 0, c],
            row_dev[way],
        )

    def zone_copy(way):
        return remote(ZS.at[way], ZR.at[way], zone_send.at[way], zone_recv.at[way], row_dev[way])

    inner = ((top + rows - 1), top)
    outer = ((top - 1), top + rows)

    def pack_rows(src, t, c, count):
        for way in range(2):
            for u in range(count):
                MS[way, t, c, u : u + 1, :] = src[c, u, inner[way] : inner[way] + 1, :]

    def unpack_rows(dst, t, c, count):
        for way in range(2):
            for u in range(count):
                dst[c, u, outer[way] : outer[way] + 1, :] = MR[way, t, c, u : u + 1, :]

    def edge_copy(c, way):
        return remote(E.at[c], EN.at[way, c], edge_send.at[way, c], edge_recv.at[way, c], col_dev[way])

    def code_copy(way):
        return remote(CO, CN.at[way], code_send.at[way], code_recv.at[way], col_dev[way])

    def y_copy(way):
        return remote(YS.at[way], YR.at[way], y_send.at[way], y_recv.at[way], y_dev[way])

    def x_copy(way):
        return remote(XS.at[way], XR.at[way], x_send.at[way], x_recv.at[way], x_dev[way])

    inner_g = (top + rows_g - 1, top)
    outer_g = (top - 1, top + rows_g)

    def z_copy(f, way):
        src, dst = ((layers_g, 0), (1, layers_g + 1))[way]
        return remote(
            G.at[f, src, :, pl.ds(top, rows_g), :],
            G.at[f, dst, :, pl.ds(top, rows_g), :],
            z_send.at[f, way],
            z_recv.at[f, way],
            col_dev[way],
        )

    has_z = (gz < nz - 1, gz > 0)

    segs = (
        (0, 0, gt, 1),
        (1, gt - 1, 1, 0),
        (-1, 0, 1, gt + 1),
    )
    parts = []
    for j in range(ny):
        r0, r1 = max(0, strip * j - SUB), min(rows_g, strip * (j + 1) + SUB)
        parts.append((0, j, r0, r1 - r0, r0 - (strip * j - SUB)))
    parts.append((1, 0, rows_g - SUB, SUB, 0))
    parts.append((-1, ny - 1, 0, SUB, strip + SUB))

    def face_pieces():
        for n, (dx, j, r0, count, d0) in enumerate(parts):
            for m, (dk, s0, tiles, t0) in enumerate(segs):
                k = ring(gy, ny, dk)
                src = GS.at[pl.ds(s0, tiles), pl.ds(r0, count), :]
                dst = GB.at[pl.ds(t0, tiles), pl.ds(d0, count), :]
                copy = remote(src, dst, face_send.at[n, m], face_recv.at[m], dev(ring(gx, nx, dx), j, k))
                me = (k == 0) & (gy == j) if dx == 0 else None
                yield copy, me, src, dst

    def face_wait(m):
        dk, _, tiles, t0 = segs[m]
        own = (gz == 0) & (ring(gy, ny, dk) == 0)

        def take(count):
            dst = GB.at[pl.ds(t0, tiles), pl.ds(0, count), :]
            remote(dst, dst, face_send.at[0, m], face_recv.at[m], y_dev[0]).wait_recv()

        @pl.when(jnp.logical_not(own))
        def _():
            take(strip + 2 * SUB)

        @pl.when(own & ((gy == 0) | (gy == ny - 1)))
        def _():
            take(SUB)

    def wt_copy():
        where = pl.ds(pl.multiple_of(gy * strip, SUB), strip)
        return remote(WS, WR.at[:, where, :], wt_send, wt_recv.at[gy], dev(gx, gz, 0))

    for k in range(gt):
        load_gas(0, temp_in, k).start()
    load_flags.start()
    for c in range(chunks):
        for k in range(wt):
            load_wall(solid_in, c, k).start()
    for k in range(gt):
        load_gas(1, fuel_in, k).start()
    load_owner.start()
    for c in range(chunks):
        for k in range(wt):
            load_wall(diff_in, c, k).start()
    load_vel.start()

    for k in range(gt):
        load_gas(0, temp_in, k).wait()
    load_flags.wait()

    @pl.when(gz == 0)
    def _():
        for k in range(gt):
            on = FL[:, k * LANES : (k + 1) * LANES].astype(jnp.float32)
            GS[k] = on * G[0, 1, k, top : top + rows_g, :]
        for copy, me, src, dst in face_pieces():
            if me is None:
                copy.start()
            else:

                @pl.when(jnp.logical_not(me))
                def _(copy=copy):
                    copy.start()

                @pl.when(me)
                def _(src=src, dst=dst):
                    dst[...] = src[...]

    def send_first(i, carry):
        c = lax.rem(i + 1, chunks)
        for k in range(wt):
            load_wall(solid_in, c, k).wait()
        pack_rows(A, 0, c, units)
        for way in range(2):
            first_copy(c, way).start()
        return carry

    lax.fori_loop(0, chunks, send_first, 0)

    for k in range(gt):
        load_gas(1, fuel_in, k).wait()
    per = SUB // (2 * gt)

    def pack_x(i, carry):
        for way in range(2):
            for f in range(2):
                for n in range(per):
                    for k in range(gt):
                        z = i * per + n
                        at = (f * per + n) * gt + k
                        XS[way, i, at : at + 1, :] = G[f, z + 1, k, inner_g[way] : inner_g[way] + 1, :]
        return carry

    lax.fori_loop(0, layers_g // per, pack_x, 0)
    for way in range(2):
        x_copy(way).start()
    for f in range(2):
        for way in range(2):

            @pl.when(has_z[way])
            def _(f=f, way=way):
                z_copy(f, way).start()

        @pl.when(gz == 0)
        def _(f=f):
            for k in range(gt):
                G[f, 0, k, top : top + rows_g, :] = G[f, 1, k, top : top + rows_g, :]

        @pl.when(gz == nz - 1)
        def _(f=f):
            for k in range(gt):
                G[f, layers_g + 1, k, top : top + rows_g, :] = G[f, layers_g, k, top : top + rows_g, :]

    for c in range(chunks):
        for k in range(wt):
            load_wall(diff_in, c, k).wait()
    group = lane // GROUP
    within = lane % GROUP
    low_half = within < 2 * HALO

    def pack_edges(i, carry):
        c = lax.rem(i + 1, chunks)
        for r in range(rtiles):
            acc = jnp.zeros((SUB, LANES), jnp.float32)
            for l in range(CHUNK):
                far = (wt - 1) * CHUNK + l
                at = slice(top + r * SUB, top + (r + 1) * SUB)
                ad = slice(r * SUB, (r + 1) * SUB)
                s = jnp.where(lane >= LANES - HALO, A[c, far, at, :], A[c, l, at, :])
                d = jnp.where(lane >= LANES - HALO, D[c, far, ad, :], D[c, l, ad, :])
                s = pltpu.roll(s, GROUP * l + HALO, 1)
                d = pltpu.roll(d, (GROUP * l + 3 * HALO) % LANES, 1)
                acc = jnp.where(group == l, jnp.where(low_half, s, d), acc)
            E[c, r * SUB : (r + 1) * SUB, :] = acc
        for way in range(2):
            edge_copy(c, way).start()
        return carry

    lax.fori_loop(0, chunks, pack_edges, 0)

    load_owner.wait()
    all_cols, all_rows = cols_g * ny, rows_g * nx

    def wrapped(x, n):
        x = jnp.where(x < 0, x + n, x)
        return jnp.where(x >= n, x - n, x)

    for r in range(rtiles):
        rr = slice(r * SUB, (r + 1) * SUB)
        p = line * strip + (r * SUB + iota((SUB, LANES), 0)) // 2
        for k in range(wt):
            q = gz * cols_g + (k * LANES + lane) // 2
            owner = OW[rr, k * LANES : (k + 1) * LANES]
            if all_cols & (all_cols - 1) == 0:
                a = lax.shift_right_logical(owner, all_cols.bit_length() - 1)
                b = owner & (all_cols - 1)
            else:
                a = lax.div(owner, all_cols)
                b = owner - a * all_cols
            down = wrapped(a - p + DISP, all_rows)
            along = wrapped(b - q + DISP, all_cols)
            OW[rr, k * LANES : (k + 1) * LANES] = down * 16 + along
        first, final = OW[rr, 0:LANES], OW[rr, cols - LANES : cols]
        CO[rr, :] = pltpu.roll(jnp.where(lane >= LANES - HALO, final, first), HALO, 1)
    for way in range(2):
        code_copy(way).start()

    def pack_cols(i, acc):
        out = list(acc)
        for n in range(4):
            z = i * 4 + n
            for f in range(2):
                k = f * layers_g + z
                for r in range(gtiles):
                    at = slice(top + r * SUB, top + (r + 1) * SUB)
                    high = pltpu.roll(G[f, z + 1, gt - 1, at, :], k + 1, 1)
                    low = pltpu.roll(G[f, z + 1, 0, at, :], k + LANES // 2, 1)
                    new = jnp.where(lane == k, high, out[r])
                    out[r] = jnp.where(lane == k + LANES // 2, low, new)
        return tuple(out)

    zero = jnp.zeros((SUB, LANES), jnp.float32)
    packed = lax.fori_loop(0, layers_g // 4, pack_cols, (zero,) * gtiles)
    half = gtiles // 2
    left_half = lane < LANES // 2
    for r in range(half):
        rr = slice(r * SUB, (r + 1) * SUB)
        near, away = packed[r], packed[r + half]
        YS[0, rr, :] = jnp.where(left_half, near, pltpu.roll(away, LANES // 2, 1))
        YS[1, rr, :] = jnp.where(left_half, pltpu.roll(near, LANES // 2, 1), away)
    for way in range(2):
        y_copy(way).start()

    def build_zone(i, carry):
        c = lax.rem(i + 1, chunks)
        for way in range(2):
            edge_copy(c, way).wait_recv()
        for r in range(rtiles):
            rr = slice(r * SUB, (r + 1) * SUB)
            mine, left, right = E[c, rr, :], EN[0, c, rr, :], EN[1, c, rr, :]
            hi = (within < HALO) | ((within >= 2 * HALO) & (within < 3 * HALO))
            a = jnp.where(hi, left, mine)
            b = jnp.where(hi, mine, right)
            zone = jnp.where(low_half, a, pltpu.roll(b, 2 * HALO, 1))
            A[c, units, top + r * SUB : top + (r + 1) * SUB, :] = zone
            D[c, units, rr, :] = jnp.where(low_half, pltpu.roll(a, LANES - 2 * HALO, 1), b)
        for way in range(2):
            ZS[way, pl.ds(c, 1), :] = A[c, units, inner[way] : inner[way] + 1, :]
        return carry

    lax.fori_loop(0, chunks, build_zone, 0)
    for way in range(2):
        zone_copy(way).start()

    load_vel.wait()

    def wall_flux():
        for m in range(len(segs)):
            face_wait(m)
        for way in range(2):
            code_copy(way).wait_recv()
        back = LANES // 4
        for m in range(wt):
            start = LANES + m * (LANES // 2) - back
            a, off = start // LANES, start % LANES
            for r in range((strip + 2 * SUB) // SUB):
                rr = slice(r * SUB, (r + 1) * SUB)
                u = pltpu.roll(GB[a, rr, :], LANES - off, 1)
                v = pltpu.roll(GB[a + 1, rr, :], LANES - off, 1)
                w = jnp.where(lane < LANES - off, u, v)
                DW[m, pl.ds(2 * r * SUB, SUB, stride=2), :] = w
                DW[m, pl.ds(2 * r * SUB + 1, SUB, stride=2), :] = w

        def pick(r, code, windows):
            row, col = lax.shift_right_logical(code, 4), code & 15
            g = jnp.zeros((SUB, LANES), jnp.float32)
            for n in range(SPAN):
                got = None
                for mask, m, base in windows:
                    u = DW[m, r * SUB + 2 * n + 2 * (SUB - DISP) : r * SUB + 2 * n + 2 * (SUB - DISP) + SUB, :]
                    x = lanes_of(u, (base + col) & (LANES - 1))
                    got = x if got is None else jnp.where(mask, got, x)
                g = jnp.where(row == n, got, g)
            return g

        def flux_of(g, surf):
            power = jnp.exp(0.7 * jnp.log(jnp.maximum(g, 1.0)))
            film = jnp.where(g > 0.0, FILM_COEF * power, 0.0)
            return SOURCE_GAIN * film * (g - surf)

        for r in range(rtiles):
            rr = slice(r * SUB, (r + 1) * SUB)
            at = slice(top + r * SUB, top + (r + 1) * SUB)
            for m in range(wt):
                base = lane // 2 + back - DISP
                g = pick(r, OW[rr, m * LANES : (m + 1) * LANES], ((None, m, base),))
                F[m, rr, :] = flux_of(g, A[0, m * CHUNK, at, :])
            mine, left, right = CO[rr, :], CN[0, rr, :], CN[1, rr, :]
            near = lane < HALO
            a = jnp.where(near, left, mine)
            b = pltpu.roll(jnp.where(near, mine, right), 2 * HALO, 1)
            code = jnp.where(lane < 2 * HALO, a, b)
            lo = lane // 2 - HALO // 2 + back - DISP
            hi = lane // 2 - HALO + cols_g - HALO // 2 - ((wt - 1) * (LANES // 2) - back) - DISP
            g = pick(r, code, ((lane < 2 * HALO, 0, lo), (lane < 2 * HALO, wt - 1, hi)))
            flux = flux_of(g, A[0, units, at, :])
            F[wt, rr, :] = jnp.where(lane < GROUP, flux, 0.0)

    def gas_layer(z):
        gi = z + 1
        for r in range(gtiles):
            base = top + r * SUB
            at = slice(base, base + SUB)
            rr = slice(r * SUB, (r + 1) * SUB)
            shift = LANES // 2 if r >= half else 0
            fold = slice((r % half) * SUB, (r % half + 1) * SUB)
            rates = []
            for f in range(2):
                c = [G[f, gi, k, at, :] for k in range(gt)]
                key = f * layers_g + z + shift
                low = pltpu.roll(YR[0, fold, :], lax.rem(LANES - key, LANES), 1)
                high = pltpu.roll(YR[1, fold, :], LANES - 1 - key, 1)
                fwd = [low] + [pltpu.roll(x, 1, 1) for x in c]
                bwd = [pltpu.roll(x, LANES - 1, 1) for x in c] + [high]
                out = []
                for k in range(gt):
                    xl = G[f, gi, k, base - 1 : base - 1 + SUB, :]
                    xh = G[f, gi, k, base + 1 : base + 1 + SUB, :]
                    zl, zh = G[f, gi - 1, k, at, :], G[f, gi + 1, k, at, :]
                    yl = jnp.where(lane == 0, fwd[k], fwd[k + 1])
                    yh = jnp.where(lane == LANES - 1, bwd[k + 1], bwd[k])
                    cs = slice(k * LANES, (k + 1) * LANES)
                    advect = V[0, z, rr, cs] * (zh - zl) + V[1, z, rr, cs] * (xh - xl) + V[2, z, rr, cs] * (yh - yl)
                    nearby = zl + zh + xl + xh + yl + yh
                    coef = DIFFUSE_TEMP if f == 0 else DIFFUSE_FUEL
                    out.append((c[k], coef * (nearby - 6.0 * c[k]) - 0.5 * advect))
                rates.append(out)
            for k in range(gt):
                cs = slice(k * LANES, (k + 1) * LANES)
                (t, t_rate), (y, y_rate) = rates[0][k], rates[1][k]
                reaction = RATE_CONST * y * jnp.exp(-ACTIVATION / t)
                TO[z, rr, cs] = t + TIME_STEP * (t_rate + HEAT_RELEASE * reaction)
                FO[z, rr, cs] = y + TIME_STEP * (y_rate - reaction)

    def wall_chunk(src, dst, c):
        first, final = c == 0, c == chunks - 1
        cb, ca = jnp.maximum(c - 1, 0), jnp.minimum(c + 1, chunks - 1)
        lb = jnp.where(first, 0, CHUNK - 1)
        for r in range(rtiles):
            base = top + r * SUB
            at = slice(base, base + SUB)
            rr = slice(r * SUB, (r + 1) * SUB)
            zone = src[c, units, at, :]
            for l in range(CHUNK):
                cs = [src[c, k * CHUNK + l, at, :] for k in range(wt)]
                left = pltpu.roll(zone, LANES - GROUP * l - HALO + 1, 1)
                right = pltpu.roll(zone, LANES - 1 - GROUP * l - 3 * HALO, 1)
                fwd = [left] + [pltpu.roll(x, 1, 1) for x in cs]
                bwd = [pltpu.roll(x, LANES - 1, 1) for x in cs] + [right]
                for k in range(wt):
                    u = k * CHUNK + l
                    below = src[c, u - 1, at, :] if l else src[cb, k * CHUNK + lb, at, :]
                    if l < CHUNK - 1:
                        above = src[c, u + 1, at, :]
                    else:
                        above = jnp.where(final, COOLANT, src[ca, k * CHUNK, at, :])
                    nearby = below + above
                    nearby = nearby + src[c, u, base - 1 : base - 1 + SUB, :]
                    nearby = nearby + src[c, u, base + 1 : base + 1 + SUB, :]
                    nearby = nearby + jnp.where(lane == 0, fwd[k], fwd[k + 1])
                    nearby = nearby + jnp.where(lane == LANES - 1, bwd[k + 1], bwd[k])
                    dst[c, u, at, :] = cs[k] + D[c, u, rr, :] * (nearby - 6.0 * cs[k])
            below = jnp.where(first, zone, pltpu.roll(src[cb, units, at, :], GROUP, 1))
            below = jnp.where(lane < GROUP, below, pltpu.roll(zone, GROUP, 1))
            above = jnp.where(final, COOLANT, pltpu.roll(src[ca, units, at, :], LANES - GROUP, 1))
            above = jnp.where(lane >= LANES - GROUP, above, pltpu.roll(zone, LANES - GROUP, 1))
            nearby = below + above
            nearby = nearby + src[c, units, base - 1 : base - 1 + SUB, :]
            nearby = nearby + src[c, units, base + 1 : base + 1 + SUB, :]
            nearby = nearby + pltpu.roll(zone, 1, 1) + pltpu.roll(zone, LANES - 1, 1)
            dst[c, units, at, :] = zone + D[c, units, rr, :] * (nearby - 6.0 * zone)

        @pl.when(first)
        def _():
            for r in range(rtiles):
                at = slice(top + r * SUB, top + (r + 1) * SUB)
                rr = slice(r * SUB, (r + 1) * SUB)
                for k in range(wt):
                    dst[0, k * CHUNK, at, :] = dst[0, k * CHUNK, at, :] + F[k, rr, :]
                dst[0, units, at, :] = dst[0, units, at, :] + F[wt, rr, :]

    def step(src, dst, u, odd, i):
        t = 2 * u + 2 - odd
        s = (t - 1) * chunks + i
        c = lax.rem(i + 1, chunks)
        z = lax.rem(s + 1, layers_g)
        if odd:

            @pl.when(s == 0)
            def _():
                for way in range(2):
                    y_copy(way).wait_recv()
                    zone_copy(way).wait_recv()
                    x_copy(way).wait_recv()
                    for f in range(2):

                        @pl.when(has_z[1 - way])
                        def _(f=f, way=way):
                            z_copy(f, way).wait_recv()

                    for n in range(chunks):
                        A[n, units, outer[way] : outer[way] + 1, :] = ZR[way, n : n + 1, :]

                def unpack_x(j, carry):
                    for way in range(2):
                        for f in range(2):
                            for n in range(per):
                                for k in range(gt):
                                    at = (f * per + n) * gt + k
                                    G[f, j * per + n + 1, k, outer_g[way] : outer_g[way] + 1, :] = XR[
                                        way, j, at : at + 1, :
                                    ]
                    return carry

                lax.fori_loop(0, layers_g // per, unpack_x, 0)

        gas_layer(z)
        store_gas(1, z).start()

        @pl.when(z > 0)
        def _():
            store_gas(0, z).start()

        if odd:

            @pl.when(u == 0)
            def _():
                for way in range(2):
                    first_copy(c, way).wait_recv()
                unpack_rows(src, 0, c, units)

            @pl.when(u > 0)
            def _():
                for way in range(2):
                    row_copy(t - 1, c, way).wait_recv()
                unpack_rows(src, t - 1, c, units + 1)

            @pl.when((u == 0) & (c == 0))
            def _():
                wall_flux()

        else:
            for way in range(2):
                row_copy(t - 1, c, way).wait_recv()
            unpack_rows(src, t - 1, c, units + 1)

        wall_chunk(src, dst, c)

        def send():
            pack_rows(dst, t, c, units + 1)
            for way in range(2):
                row_copy(t, c, way).start()

        if odd:
            send()
        else:
            pl.when(t < SUBSTEPS)(send)

            @pl.when(t == SUBSTEPS)
            def _():
                for k in range(wt):
                    store_wall(c, k).start()

    def two_steps(u, carry):
        for odd, src, dst in ((1, A, B), (0, B, A)):

            def body(i, inner_carry, odd=odd, src=src, dst=dst):
                step(src, dst, u, odd, i)
                return inner_carry

            lax.fori_loop(0, chunks, body, 0)
        return carry

    lax.fori_loop(0, SUBSTEPS // 2, two_steps, 0)

    for r in range(strip // SUB):
        pairs = []
        for k in range(wt):
            base = top + 2 * r * SUB
            x = A[0, k * CHUNK, pl.ds(base, SUB, stride=2), :] + A[0, k * CHUNK, pl.ds(base + 1, SUB, stride=2), :]
            pairs.append(0.25 * (x + pltpu.roll(x, LANES - 1, 1)))
        idx = (2 * lane) & (LANES - 1)
        for k in range(gt):
            a, b = lanes_of(pairs[2 * k], idx), lanes_of(pairs[2 * k + 1], idx)
            WS[k, r * SUB : (r + 1) * SUB, :] = jnp.where(lane < LANES // 2, a, b)
    self_tile = (gz == 0) & (gy == 0)

    @pl.when(jnp.logical_not(self_tile))
    def _():
        wt_copy().start()

    @pl.when(self_tile)
    def _():
        WR[:, 0:strip, :] = WS[...]

    @pl.when(gz == 0)
    def _():
        for j in range(ny):
            where = pl.ds(j * strip, strip)

            def take(where=where, j=j):
                remote(WS, WR.at[:, where, :], wt_send, wt_recv.at[j], y_dev[0]).wait_recv()

            if j == 0:
                pl.when(gy > 0)(take)
            else:
                take()
        for k in range(gt):
            cs = slice(k * LANES, (k + 1) * LANES)
            gap = jnp.where(FL[:, cs] == 1, 2.0 * (WR[k] - G[0, 1, k, top : top + rows_g, :]), 0.0)
            TO[0, :, cs] = TO[0, :, cs] + TIME_STEP * (0.5 * V[0, 0, :, cs] + DIFFUSE_TEMP) * gap

    store_gas(0, 0).start()

    @pl.when(gz == 0)
    def _():
        for copy, me, _, _ in face_pieces():
            if me is None:
                copy.wait_send()
            else:
                pl.when(jnp.logical_not(me))(copy.wait_send)

    pl.when(jnp.logical_not(self_tile))(lambda: wt_copy().wait_send())
    for way in range(2):
        code_copy(way).wait_send()
        y_copy(way).wait_send()
        zone_copy(way).wait_send()
        x_copy(way).wait_send()
        for f in range(2):

            @pl.when(has_z[way])
            def _(f=f, way=way):
                z_copy(f, way).wait_send()

    def drain(c, carry):
        for way in range(2):
            edge_copy(c, way).wait_send()
            first_copy(c, way).wait_send()
            for t in range(1, SUBSTEPS):
                row_copy(t, c, way).wait_send()
        for k in range(wt):
            store_wall(c, k).wait()
        return carry

    lax.fori_loop(0, chunks, drain, 0)

    def drain_gas(z, carry):
        store_gas(0, z).wait()
        store_gas(1, z).wait()
        return carry

    lax.fori_loop(0, layers_g, drain_gas, 0)


def shards(mesh_shape, gas_temp, fuel_frac, velocity, wall_flags, solid_temp, diffusivity, gas_owner):
    nx, ny, nz = mesh_shape
    layers_g, rows_g, cols_g = gas_temp.shape
    layers, rows, cols = solid_temp.shape
    chunks, wt, gt = layers // CHUNK, cols // LANES, cols_g // LANES
    units = wt * CHUNK
    strip = rows // 2
    assert ny == nz and cols == 2 * cols_g and rows * ny == 2 * rows_g
    assert layers_g == SUBSTEPS * chunks and 2 * layers_g <= LANES // 2 and chunks * wt >= layers_g
    assert wt == 2 * gt and gt == 2 and layers % CHUNK == 0
    f32, i32 = jnp.float32, jnp.int32
    dma = pltpu.SemaphoreType.DMA
    scratch = [
        pltpu.VMEM((2, layers_g + 2, gt, rows_g + 2 * SUB, LANES), f32),
        pltpu.VMEM((3, layers_g, rows_g, cols_g), f32),
        pltpu.VMEM((rows_g, cols_g), i32),
        pltpu.VMEM((chunks, units + 1, rows + 2 * SUB, LANES), f32),
        pltpu.VMEM((chunks, units + 1, rows + 2 * SUB, LANES), f32),
        pltpu.VMEM((chunks, units + 1, rows, LANES), f32),
        pltpu.VMEM((layers_g, rows_g, cols_g), f32),
        pltpu.VMEM((layers_g, rows_g, cols_g), f32),
        pltpu.VMEM((rows, cols), i32),
        pltpu.VMEM((chunks, rows, LANES), f32),
        pltpu.VMEM((2, chunks, rows, LANES), f32),
        pltpu.VMEM((rows, LANES), i32),
        pltpu.VMEM((2, rows, LANES), i32),
        pltpu.VMEM((2, SUBSTEPS, chunks, units + SUB, LANES), f32),
        pltpu.VMEM((2, SUBSTEPS, chunks, units + SUB, LANES), f32),
        pltpu.VMEM((2, chunks, LANES), f32),
        pltpu.VMEM((2, chunks, LANES), f32),
        pltpu.VMEM((2, layers_g * 2 * gt // SUB, SUB, LANES), f32),
        pltpu.VMEM((2, layers_g * 2 * gt // SUB, SUB, LANES), f32),
        pltpu.VMEM((2, rows_g // 2, LANES), f32),
        pltpu.VMEM((2, rows_g // 2, LANES), f32),
        pltpu.VMEM((gt, rows_g, LANES), f32),
        pltpu.VMEM((gt + 2, strip + 2 * SUB, LANES), f32),
        pltpu.VMEM((wt, 2 * (strip + 2 * SUB), LANES), f32),
        pltpu.VMEM((wt + 1, rows, LANES), f32),
        pltpu.VMEM((gt, strip, LANES), f32),
        pltpu.VMEM((gt, rows_g, LANES), f32),
        dma((chunks, wt)),
        dma((chunks, wt)),
        dma((2, gt)),
        dma((3,)),
        dma((3, chunks, wt)),
        dma((2, SUBSTEPS, chunks)),
        dma((2, SUBSTEPS, chunks)),
        dma((2,)),
        dma((2,)),
        dma((2, chunks)),
        dma((2, chunks)),
        dma((2,)),
        dma((2,)),
        dma((2,)),
        dma((2,)),
        dma((2,)),
        dma((2,)),
        dma((2, 2)),
        dma((2, 2)),
        dma((ny + 2, 3)),
        dma((3,)),
        dma(()),
        dma((ny,)),
    ]
    return pl.pallas_call(
        functools.partial(mega_kernel, mesh_shape),
        out_shape=(
            jax.ShapeDtypeStruct(gas_temp.shape, f32),
            jax.ShapeDtypeStruct(fuel_frac.shape, f32),
            jax.ShapeDtypeStruct(solid_temp.shape, f32),
        ),
        in_specs=[ANY] * 7,
        out_specs=(ANY,) * 3,
        scratch_shapes=scratch,
        compiler_params=pltpu.CompilerParams(vmem_limit_bytes=60 << 20, has_side_effects=True),
        cost_estimate=pl.CostEstimate(flops=200_000_000, bytes_accessed=26 << 20, transcendentals=1 << 19),
        name="section",
    )(gas_temp, fuel_frac, velocity, wall_flags, solid_temp, diffusivity, gas_owner)


def solution(mesh):
    placed = (
        P("gz", "gx", "gy"),
        P("gz", "gx", "gy"),
        P(None, "gz", "gx", "gy"),
        P("gx", "gy"),
        P(None, ("gx", "gy"), "gz"),
        P(None, ("gx", "gy"), "gz"),
        P(("gx", "gy"), "gz"),
    )
    mesh_shape = tuple(mesh.shape[a] for a in ("gx", "gy", "gz"))
    return jax.shard_map(
        functools.partial(shards, mesh_shape),
        mesh=mesh,
        in_specs=placed,
        out_specs=(P("gz", "gx", "gy"), P("gz", "gx", "gy"), P(None, ("gx", "gy"), "gz")),
        check_vma=False,
    )
```

time: 175 us -> 63.2 us (0.36)
  the two profiles are of different devices: /device:TPU:28 before, /device:TPU:0 now
where the time goes in v1:
time: 63.2 us; the launch traced here: 63 us
  Pallas kernels  54.2 us (86%)
  local copies, waits for them, and re-layouts  8.24 us (13%)
  between operations  0.65 us (1%)
    pallas_call x1, Pallas kernels, shards(): pl.pallas_call(functools.partial(mega_kernel, mesh_shape), out_shape=(jax...  54.2 us
    unnamed x7, local copies, waits for them, and re-layouts  8.24 us

profile of v1, /device:TPU:0, one launch (start us, length us, event | category | flops | bytes accessed | tf_op | source)
XLA Modules:
  0.0 63.0 jit_solution(4402652966850546790)
XLA Ops:
  0.6 54.2 %section.1 = (f32[32,64,256]{2,1,0:T(8,128)}, f32[32,64,256]{2,1,0:T(8,128)}, f32[64,32,512]{2,1,0:T(8,128)}) custom-call(f32[32,64,256]{2,1,0:T(8,128)} %temp_in.1, f32[32,64,256]{2,1,0:T(8,128)} %fuel_in.1, f32[3,32,64,256]{3,2,1,0:T(8,128)} %vel_in.1, s32[64,256]{1,0:T(8,128)} %flags_in.1, f32[64,32,512]{2,1,0:T(8,128)} %solid_in.1, ...), custom_call_target="tpu_custom_call" | custom-call | flops 200000000 | bytes 27262976 | tf_op jit(solution)/shard_map/section/pallas_call | solution.py:832
  54.8 0.0 copy-start.1
  54.8 3.3 %copy.13 = f32[32,64,256]{2,1,0:T(8,128)} copy(f32[32,64,256]{2,1,0:T(8,128)} %get-tuple-element.6) | data formatting | bytes 4194304
  58.1 0.0 copy-done.1
  58.1 0.0 copy-start
  58.1 1.3 %copy.14 = f32[32,64,256]{2,1,0:T(8,128)} copy(f32[32,64,256]{2,1,0:T(8,128)S(1)} %copy-done.1) | data formatting | bytes 4194304
  59.4 1.6 %copy-done = f32[64,32,512]{2,1,0:T(8,128)S(1)} copy-done((f32[64,32,512]{2,1,0:T(8,128)S(1)}, f32[64,32,512]{2,1,0:T(8,128)}, u32[]{:S(2)}) %copy-start) | copy-done | bytes 4194328
  61.0 2.0 %copy.15 = f32[64,32,512]{2,1,0:T(8,128)} copy(f32[64,32,512]{2,1,0:T(8,128)S(1)} %copy-done) | data formatting | bytes 8388608
Async XLA Ops:
  54.8 3.3 %copy-start.1 = (f32[32,64,256]{2,1,0:T(8,128)S(1)}, f32[32,64,256]{2,1,0:T(8,128)}, u32[]{:S(2)}) copy-start(f32[32,64,256]{2,1,0:T(8,128)} %get-tuple-element.7) | copy-start | bytes 6291460
  58.1 2.9 %copy-start = (f32[64,32,512]{2,1,0:T(8,128)S(1)}, f32[64,32,512]{2,1,0:T(8,128)}, u32[]{:S(2)}) copy-start(f32[64,32,512]{2,1,0:T(8,128)} %get-tuple-element.8) | copy-start | bytes 12582916

commit v2 on v1

--- a/solution.py
+++ b/solution.py
@@ -26,8 +26,10 @@
 GROUP = LANES // CHUNK
 HALO = SUBSTEPS
 SPAN = 2 * DISP + 1
+PIECES = 4
 MESH = pl.DeviceIdType.MESH
 ANY = pl.BlockSpec(memory_space=pl.ANY)
+VMEM = pl.BlockSpec(memory_space=pltpu.VMEM)
 
 
 def iota(shape, dim):
@@ -47,17 +49,15 @@
     solid_in,
     diff_in,
     owner_in,
-    temp_out,
-    fuel_out,
-    solid_out,
+    TO,
+    FO,
+    SO,
     G,
     V,
     FL,
     A,
     B,
     D,
-    TO,
-    FO,
     OW,
     E,
     EN,
@@ -75,13 +75,13 @@
     GB,
     DW,
     F,
+    L0,
     WS,
     WR,
     load_s,
     load_d,
     load_g,
     load_m,
-    out_sem,
     row_send,
     row_recv,
     zone_send,
@@ -157,17 +157,6 @@
     load_owner = pltpu.make_async_copy(owner_in, OW, load_m.at[1])
     load_vel = pltpu.make_async_copy(vel_in, V, load_m.at[2])
 
-    def store_wall(c, k):
-        return pltpu.make_async_copy(
-            A.at[c, pl.ds(k * CHUNK, CHUNK), pl.ds(top, rows), :],
-            solid_out.at[pl.ds(c * CHUNK, CHUNK), :, pl.ds(k * LANES, LANES)],
-            out_sem.at[2, c, k],
-        )
-
-    def store_gas(f, z):
-        src, dst = ((TO, temp_out), (FO, fuel_out))[f]
-        return pltpu.make_async_copy(src.at[z], dst.at[z], out_sem.at[f, lax.div(z, wt), lax.rem(z, wt)])
-
     def row_copy(t, c, way):
         count = pl.ds(0, units + 1)
         return remote(
@@ -188,21 +177,35 @@
             row_dev[way],
         )
 
-    def zone_copy(way):
-        return remote(ZS.at[way], ZR.at[way], zone_send.at[way], zone_recv.at[way], row_dev[way])
+    diag_dev = tuple(
+        tuple(dev(x, y, ring(gz, nz, by)) for by in (1, 0, -1)) for x, y, _ in row_dev
+    )
+
+    def zone_copy(way, n):
+        return remote(ZS.at[way], ZR.at[way, n], zone_send.at[way, n], zone_recv.at[way, n], diag_dev[way][n])
 
     inner = ((top + rows - 1), top)
     outer = ((top - 1), top + rows)
 
-    def pack_rows(src, t, c, count):
-        for way in range(2):
-            for u in range(count):
-                MS[way, t, c, u : u + 1, :] = src[c, u, inner[way] : inner[way] + 1, :]
-
-    def unpack_rows(dst, t, c, count):
-        for way in range(2):
-            for u in range(count):
-                dst[c, u, outer[way] : outer[way] + 1, :] = MR[way, t, c, u : u + 1, :]
+    tall = rows + 2 * SUB
+    flat_a, flat_b = (x.reshape(chunks * (units + 1) * tall, LANES) for x in (A, B))
+
+    def column(c, k, row):
+        return pl.ds((c * (units + 1) + k * CHUNK) * tall + row, CHUNK, stride=tall)
+
+    def pack_rows(src, t, c, zone):
+        for way in range(2):
+            for k in range(wt):
+                MS[way, t, c, k * CHUNK : (k + 1) * CHUNK, :] = (flat_a if src is A else flat_b)[column(c, k, inner[way]), :]
+            if zone:
+                MS[way, t, c, units : units + 1, :] = src[c, units, inner[way] : inner[way] + 1, :]
+
+    def unpack_rows(dst, t, c, zone):
+        for way in range(2):
+            for k in range(wt):
+                (flat_a if dst is A else flat_b)[column(c, k, outer[way]), :] = MR[way, t, c, k * CHUNK : (k + 1) * CHUNK, :]
+            if zone:
+                dst[c, units, outer[way] : outer[way] + 1, :] = MR[way, t, c, units : units + 1, :]
 
     def edge_copy(c, way):
         return remote(E.at[c], EN.at[way, c], edge_send.at[way, c], edge_recv.at[way, c], col_dev[way])
@@ -238,10 +241,10 @@
     )
     parts = []
     for j in range(ny):
-        r0, r1 = max(0, strip * j - SUB), min(rows_g, strip * (j + 1) + SUB)
-        parts.append((0, j, r0, r1 - r0, r0 - (strip * j - SUB)))
-    parts.append((1, 0, rows_g - SUB, SUB, 0))
-    parts.append((-1, ny - 1, 0, SUB, strip + SUB))
+        r0, r1 = max(0, strip * j - DISP), min(rows_g, strip * (j + 1) + DISP)
+        parts.append((0, j, r0, r1 - r0, r0 - (strip * j - DISP)))
+    parts.append((1, 0, rows_g - DISP, DISP, 0))
+    parts.append((-1, ny - 1, 0, DISP, strip + DISP))
 
     def face_pieces():
         for n, (dx, j, r0, count, d0) in enumerate(parts):
@@ -263,106 +266,86 @@
 
         @pl.when(jnp.logical_not(own))
         def _():
-            take(strip + 2 * SUB)
+            take(strip + 2 * DISP)
 
         @pl.when(own & ((gy == 0) | (gy == ny - 1)))
         def _():
-            take(SUB)
+            take(DISP)
 
     def wt_copy():
         where = pl.ds(pl.multiple_of(gy * strip, SUB), strip)
         return remote(WS, WR.at[:, where, :], wt_send, wt_recv.at[gy], dev(gx, gz, 0))
 
+    def load_face(k):
+        return pltpu.make_async_copy(temp_in.at[0, :, pl.ds(k * LANES, LANES)], GS.at[k], load_m.at[3 + k])
+
+    def start_wall(src):
+        def body(i, carry):
+            c = lax.rem(i + 1, chunks)
+            for k in range(wt):
+                load_wall(src, c, k).start()
+            return carry
+
+        lax.fori_loop(0, chunks, body, 0)
+
+    barrier = pltpu.get_barrier_semaphore()
+
+    def greet(to):
+        pl.semaphore_signal(barrier, inc=1, device_id=to, device_id_type=MESH)
+
+    for pair in (row_dev, col_dev, y_dev, x_dev):
+        for to in pair:
+            greet(to)
+    for x, _, y in diag_dev:
+        greet(x)
+        greet(y)
+    for dk in (0, 1, -1):
+        k = ring(gz, ny, -dk)
+        for dx, ask in ((0, None), (1, gy == ny - 1), (-1, gy == 0)):
+            to = dev(ring(gx, nx, dx), k, 0)
+            if dx == 0:
+                ask = jnp.logical_not((gz == 0) & (gy == k))
+            pl.when(ask)(functools.partial(greet, to))
+    self_tile = (gz == 0) & (gy == 0)
+
+    @pl.when(gz == 0)
+    def _():
+        for j in range(ny):
+            pl.when(jnp.logical_not((gy == 0) & (j == 0)))(functools.partial(greet, dev(gx, j, gy)))
+
+    load_flags.start()
+    for k in range(gt):
+        load_face(k).start()
+    load_owner.start()
+    start_wall(solid_in)
+    start_wall(diff_in)
     for k in range(gt):
         load_gas(0, temp_in, k).start()
-    load_flags.start()
-    for c in range(chunks):
-        for k in range(wt):
-            load_wall(solid_in, c, k).start()
     for k in range(gt):
         load_gas(1, fuel_in, k).start()
-    load_owner.start()
-    for c in range(chunks):
-        for k in range(wt):
-            load_wall(diff_in, c, k).start()
     load_vel.start()
 
+    load_flags.wait()
     for k in range(gt):
-        load_gas(0, temp_in, k).wait()
-    load_flags.wait()
-
-    @pl.when(gz == 0)
-    def _():
-        for k in range(gt):
-            on = FL[:, k * LANES : (k + 1) * LANES].astype(jnp.float32)
-            GS[k] = on * G[0, 1, k, top : top + rows_g, :]
-        for copy, me, src, dst in face_pieces():
-            if me is None:
-                copy.start()
-            else:
-
-                @pl.when(jnp.logical_not(me))
-                def _(copy=copy):
-                    copy.start()
-
-                @pl.when(me)
-                def _(src=src, dst=dst):
-                    dst[...] = src[...]
-
-    def send_first(i, carry):
+        load_face(k).wait()
+        GS[k] = GS[k] * FL[:, k * LANES : (k + 1) * LANES].astype(jnp.float32)
+
+    def pack_first(i, carry):
         c = lax.rem(i + 1, chunks)
         for k in range(wt):
             load_wall(solid_in, c, k).wait()
-        pack_rows(A, 0, c, units)
-        for way in range(2):
-            first_copy(c, way).start()
+        pack_rows(A, 0, c, False)
         return carry
 
-    lax.fori_loop(0, chunks, send_first, 0)
-
-    for k in range(gt):
-        load_gas(1, fuel_in, k).wait()
-    per = SUB // (2 * gt)
-
-    def pack_x(i, carry):
-        for way in range(2):
-            for f in range(2):
-                for n in range(per):
-                    for k in range(gt):
-                        z = i * per + n
-                        at = (f * per + n) * gt + k
-                        XS[way, i, at : at + 1, :] = G[f, z + 1, k, inner_g[way] : inner_g[way] + 1, :]
-        return carry
-
-    lax.fori_loop(0, layers_g // per, pack_x, 0)
-    for way in range(2):
-        x_copy(way).start()
-    for f in range(2):
-        for way in range(2):
-
-            @pl.when(has_z[way])
-            def _(f=f, way=way):
-                z_copy(f, way).start()
-
-        @pl.when(gz == 0)
-        def _(f=f):
-            for k in range(gt):
-                G[f, 0, k, top : top + rows_g, :] = G[f, 1, k, top : top + rows_g, :]
-
-        @pl.when(gz == nz - 1)
-        def _(f=f):
-            for k in range(gt):
-                G[f, layers_g + 1, k, top : top + rows_g, :] = G[f, layers_g, k, top : top + rows_g, :]
-
-    for c in range(chunks):
-        for k in range(wt):
-            load_wall(diff_in, c, k).wait()
+    lax.fori_loop(0, chunks, pack_first, 0)
     group = lane // GROUP
     within = lane % GROUP
     low_half = within < 2 * HALO
 
     def pack_edges(i, carry):
-        c = lax.rem(i + 1, chunks)
+        c = i
+        for k in range(wt):
+            load_wall(diff_in, c, k).wait()
         for r in range(rtiles):
             acc = jnp.zeros((SUB, LANES), jnp.float32)
             for l in range(CHUNK):
@@ -375,8 +358,8 @@
                 d = pltpu.roll(d, (GROUP * l + 3 * HALO) % LANES, 1)
                 acc = jnp.where(group == l, jnp.where(low_half, s, d), acc)
             E[c, r * SUB : (r + 1) * SUB, :] = acc
-        for way in range(2):
-            edge_copy(c, way).start()
+        for way, row in ((0, rows - 1), (1, 0)):
+            ZS[way, pl.ds(c, 1), :] = E[c, row : row + 1, :]
         return carry
 
     lax.fori_loop(0, chunks, pack_edges, 0)
@@ -405,8 +388,81 @@
             OW[rr, k * LANES : (k + 1) * LANES] = down * 16 + along
         first, final = OW[rr, 0:LANES], OW[rr, cols - LANES : cols]
         CO[rr, :] = pltpu.roll(jnp.where(lane >= LANES - HALO, final, first), HALO, 1)
+
+    mine = (gy == 0) | (gy == 1) | (gy == ny - 1)
+    greeted = 12 + jnp.where(self_tile, 0, 1) + jnp.where(gz == 0, jnp.where(mine, 3 * ny + 5, 3 * ny + 6), 0)
+    pl.semaphore_wait(barrier, greeted)
+
+    def send_edges(c, carry):
+        for way in range(2):
+            edge_copy(c, way).start()
+        return carry
+
+    lax.fori_loop(0, chunks, send_edges, 0)
     for way in range(2):
+        for n in range(3):
+            zone_copy(way, n).start()
         code_copy(way).start()
+
+    def send_first(i, carry):
+        c = lax.rem(i + 1, chunks)
+        for way in range(2):
+            first_copy(c, way).start()
+        return carry
+
+    lax.fori_loop(0, chunks // 2, send_first, 0)
+
+    @pl.when(gz == 0)
+    def _():
+        for copy, me, src, dst in face_pieces():
+            if me is None:
+                copy.start()
+            else:
+
+                @pl.when(jnp.logical_not(me))
+                def _(copy=copy):
+                    copy.start()
+
+                @pl.when(me)
+                def _(src=src, dst=dst):
+                    dst[...] = src[...]
+
+    lax.fori_loop(chunks // 2, chunks, send_first, 0)
+
+    for k in range(gt):
+        load_gas(0, temp_in, k).wait()
+        load_gas(1, fuel_in, k).wait()
+    per = SUB // (2 * gt)
+
+    def pack_x(i, carry):
+        for way in range(2):
+            for f in range(2):
+                for n in range(per):
+                    for k in range(gt):
+                        z = i * per + n
+                        at = (f * per + n) * gt + k
+                        XS[way, i, at : at + 1, :] = G[f, z + 1, k, inner_g[way] : inner_g[way] + 1, :]
+        return carry
+
+    lax.fori_loop(0, layers_g // per, pack_x, 0)
+    for way in range(2):
+        x_copy(way).start()
+    for f in range(2):
+        for way in range(2):
+
+            @pl.when(has_z[way])
+            def _(f=f, way=way):
+                z_copy(f, way).start()
+
+        @pl.when(gz == 0)
+        def _(f=f):
+            for k in range(gt):
+                G[f, 0, k, top : top + rows_g, :] = G[f, 1, k, top : top + rows_g, :]
+
+        @pl.when(gz == nz - 1)
+        def _(f=f):
+            for k in range(gt):
+                G[f, layers_g + 1, k, top : top + rows_g, :] = G[f, layers_g, k, top : top + rows_g, :]
 
     def pack_cols(i, acc):
         out = list(acc)
@@ -434,28 +490,31 @@
     for way in range(2):
         y_copy(way).start()
 
-    def build_zone(i, carry):
-        c = lax.rem(i + 1, chunks)
+    hi = (within < HALO) | ((within >= 2 * HALO) & (within < 3 * HALO))
+
+    def zone_of(mine, left, right):
+        a = jnp.where(hi, left, mine)
+        b = jnp.where(hi, mine, right)
+        state = jnp.where(low_half, a, pltpu.roll(b, 2 * HALO, 1))
+        return state, jnp.where(low_half, pltpu.roll(a, LANES - 2 * HALO, 1), b)
+
+    def build_zone(c):
         for way in range(2):
             edge_copy(c, way).wait_recv()
         for r in range(rtiles):
             rr = slice(r * SUB, (r + 1) * SUB)
-            mine, left, right = E[c, rr, :], EN[0, c, rr, :], EN[1, c, rr, :]
-            hi = (within < HALO) | ((within >= 2 * HALO) & (within < 3 * HALO))
-            a = jnp.where(hi, left, mine)
-            b = jnp.where(hi, mine, right)
-            zone = jnp.where(low_half, a, pltpu.roll(b, 2 * HALO, 1))
-            A[c, units, top + r * SUB : top + (r + 1) * SUB, :] = zone
-            D[c, units, rr, :] = jnp.where(low_half, pltpu.roll(a, LANES - 2 * HALO, 1), b)
-        for way in range(2):
-            ZS[way, pl.ds(c, 1), :] = A[c, units, inner[way] : inner[way] + 1, :]
-        return carry
-
-    lax.fori_loop(0, chunks, build_zone, 0)
-    for way in range(2):
-        zone_copy(way).start()
-
-    load_vel.wait()
+            state, coef = zone_of(E[c, rr, :], EN[0, c, rr, :], EN[1, c, rr, :])
+            A[c, units, top + r * SUB : top + (r + 1) * SUB, :] = state
+            D[c, units, rr, :] = coef
+
+    def zone_rows():
+        for way in range(2):
+            for n in range(3):
+                zone_copy(way, n).wait_recv()
+            state, _ = zone_of(ZR[way, 1], ZR[way, 0], ZR[way, 2])
+            ZR[way, 1] = state
+            for n in range(chunks):
+                A[n, units, outer[way] : outer[way] + 1, :] = ZR[way, 1, n : n + 1, :]
 
     def wall_flux():
         for m in range(len(segs)):
@@ -466,7 +525,7 @@
         for m in range(wt):
             start = LANES + m * (LANES // 2) - back
             a, off = start // LANES, start % LANES
-            for r in range((strip + 2 * SUB) // SUB):
+            for r in range((strip + 2 * DISP) // SUB):
                 rr = slice(r * SUB, (r + 1) * SUB)
                 u = pltpu.roll(GB[a, rr, :], LANES - off, 1)
                 v = pltpu.roll(GB[a + 1, rr, :], LANES - off, 1)
@@ -480,7 +539,7 @@
             for n in range(SPAN):
                 got = None
                 for mask, m, base in windows:
-                    u = DW[m, r * SUB + 2 * n + 2 * (SUB - DISP) : r * SUB + 2 * n + 2 * (SUB - DISP) + SUB, :]
+                    u = DW[m, r * SUB + 2 * n : r * SUB + 2 * n + SUB, :]
                     x = lanes_of(u, (base + col) & (LANES - 1))
                     got = x if got is None else jnp.where(mask, got, x)
                 g = jnp.where(row == n, got, g)
@@ -545,11 +604,11 @@
                 TO[z, rr, cs] = t + TIME_STEP * (t_rate + HEAT_RELEASE * reaction)
                 FO[z, rr, cs] = y + TIME_STEP * (y_rate - reaction)
 
-    def wall_chunk(src, dst, c):
+    def wall_chunk(src, dst, c, last, tiles):
         first, final = c == 0, c == chunks - 1
         cb, ca = jnp.maximum(c - 1, 0), jnp.minimum(c + 1, chunks - 1)
         lb = jnp.where(first, 0, CHUNK - 1)
-        for r in range(rtiles):
+        for r in tiles:
             base = top + r * SUB
             at = slice(base, base + SUB)
             rr = slice(r * SUB, (r + 1) * SUB)
@@ -572,7 +631,13 @@
                     nearby = nearby + src[c, u, base + 1 : base + 1 + SUB, :]
                     nearby = nearby + jnp.where(lane == 0, fwd[k], fwd[k + 1])
                     nearby = nearby + jnp.where(lane == LANES - 1, bwd[k + 1], bwd[k])
-                    dst[c, u, at, :] = cs[k] + D[c, u, rr, :] * (nearby - 6.0 * cs[k])
+                    new = cs[k] + D[c, u, rr, :] * (nearby - 6.0 * cs[k])
+                    if last:
+                        SO[c * CHUNK + l, rr, k * LANES : (k + 1) * LANES] = new
+                    else:
+                        dst[c, u, at, :] = new
+            if last:
+                continue
             below = jnp.where(first, zone, pltpu.roll(src[cb, units, at, :], GROUP, 1))
             below = jnp.where(lane < GROUP, below, pltpu.roll(zone, GROUP, 1))
             above = jnp.where(final, COOLANT, pltpu.roll(src[ca, units, at, :], LANES - GROUP, 1))
@@ -585,126 +650,110 @@
 
         @pl.when(first)
         def _():
-            for r in range(rtiles):
+            for r in tiles:
                 at = slice(top + r * SUB, top + (r + 1) * SUB)
                 rr = slice(r * SUB, (r + 1) * SUB)
                 for k in range(wt):
-                    dst[0, k * CHUNK, at, :] = dst[0, k * CHUNK, at, :] + F[k, rr, :]
-                dst[0, units, at, :] = dst[0, units, at, :] + F[wt, rr, :]
-
-    def step(src, dst, u, odd, i):
-        t = 2 * u + 2 - odd
-        s = (t - 1) * chunks + i
-        c = lax.rem(i + 1, chunks)
-        z = lax.rem(s + 1, layers_g)
-        if odd:
-
-            @pl.when(s == 0)
+                    if last:
+                        cs = slice(k * LANES, (k + 1) * LANES)
+                        new = SO[0, rr, cs] + F[k, rr, :]
+                        SO[0, rr, cs] = new
+                        L0[k, rr, :] = new
+                    else:
+                        dst[0, k * CHUNK, at, :] = dst[0, k * CHUNK, at, :] + F[k, rr, :]
+                if not last:
+                    dst[0, units, at, :] = dst[0, units, at, :] + F[wt, rr, :]
+
+    def gas_edges():
+        load_vel.wait()
+        for way in range(2):
+            y_copy(way).wait_recv()
+            x_copy(way).wait_recv()
+            for f in range(2):
+
+                @pl.when(has_z[1 - way])
+                def _(f=f, way=way):
+                    z_copy(f, way).wait_recv()
+
+        def unpack_x(j, carry):
+            for way in range(2):
+                for f in range(2):
+                    for n in range(per):
+                        for k in range(gt):
+                            at = (f * per + n) * gt + k
+                            G[f, j * per + n + 1, k, outer_g[way] : outer_g[way] + 1, :] = XR[
+                                way, j, at : at + 1, :
+                            ]
+            return carry
+
+        lax.fori_loop(0, layers_g // per, unpack_x, 0)
+
+    def wall_mean():
+        for r in range(strip // SUB):
+            pairs = []
+            for k in range(wt):
+                base = 2 * r * SUB
+                x = L0[k, pl.ds(base, SUB, stride=2), :] + L0[k, pl.ds(base + 1, SUB, stride=2), :]
+                pairs.append(0.25 * (x + pltpu.roll(x, LANES - 1, 1)))
+            idx = (2 * lane) & (LANES - 1)
+            for k in range(gt):
+                a, b = lanes_of(pairs[2 * k], idx), lanes_of(pairs[2 * k + 1], idx)
+                WS[k, r * SUB : (r + 1) * SUB, :] = jnp.where(lane < LANES // 2, a, b)
+
+        @pl.when(jnp.logical_not(self_tile))
+        def _():
+            wt_copy().start()
+
+        @pl.when(self_tile)
+        def _():
+            WR[:, 0:strip, :] = WS[...]
+
+    surface_at = tuple(chunks - 2 - 2 * t for t in range(SUBSTEPS))
+    gas_at = (0, 1, 2, 1)
+
+    def step(src, dst, t, i):
+        at = surface_at[t - 1]
+        c = jnp.where(i < at, i + 1, jnp.where(i == at, 0, i))
+        if t == 1:
+
+            @pl.when(i == 0)
             def _():
-                for way in range(2):
-                    y_copy(way).wait_recv()
-                    zone_copy(way).wait_recv()
-                    x_copy(way).wait_recv()
-                    for f in range(2):
-
-                        @pl.when(has_z[1 - way])
-                        def _(f=f, way=way):
-                            z_copy(f, way).wait_recv()
-
-                    for n in range(chunks):
-                        A[n, units, outer[way] : outer[way] + 1, :] = ZR[way, n : n + 1, :]
-
-                def unpack_x(j, carry):
-                    for way in range(2):
-                        for f in range(2):
-                            for n in range(per):
-                                for k in range(gt):
-                                    at = (f * per + n) * gt + k
-                                    G[f, j * per + n + 1, k, outer_g[way] : outer_g[way] + 1, :] = XR[
-                                        way, j, at : at + 1, :
-                                    ]
-                    return carry
-
-                lax.fori_loop(0, layers_g // per, unpack_x, 0)
-
-        gas_layer(z)
-        store_gas(1, z).start()
-
-        @pl.when(z > 0)
-        def _():
-            store_gas(0, z).start()
-
-        if odd:
-
-            @pl.when(u == 0)
+                for n in range(3):
+                    build_zone(n)
+                zone_rows()
+
+            @pl.when((c > 1) & (c < chunks - 1))
             def _():
-                for way in range(2):
-                    first_copy(c, way).wait_recv()
-                unpack_rows(src, 0, c, units)
-
-            @pl.when(u > 0)
-            def _():
-                for way in range(2):
-                    row_copy(t - 1, c, way).wait_recv()
-                unpack_rows(src, t - 1, c, units + 1)
-
-            @pl.when((u == 0) & (c == 0))
-            def _():
-                wall_flux()
-
-        else:
-            for way in range(2):
-                row_copy(t - 1, c, way).wait_recv()
-            unpack_rows(src, t - 1, c, units + 1)
-
-        wall_chunk(src, dst, c)
-
-        def send():
-            pack_rows(dst, t, c, units + 1)
+                build_zone(c + 1)
+
+        if t == 2:
+            pl.when(i == 0)(gas_edges)
+        for n in range(gas_at[t - 1]):
+            done = sum(gas_at[: t - 1]) * chunks + i * gas_at[t - 1] + n
+            gas_layer(lax.rem(done + 1, layers_g))
+        for way in range(2):
+            (first_copy(c, way) if t == 1 else row_copy(t - 1, c, way)).wait_recv()
+        unpack_rows(src, t - 1, c, t > 1)
+        if t == 1:
+            pl.when(c == 0)(wall_flux)
+        if t < SUBSTEPS:
+            wall_chunk(src, dst, c, False, (0, rtiles - 1))
+            pack_rows(dst, t, c, True)
             for way in range(2):
                 row_copy(t, c, way).start()
-
-        if odd:
-            send()
+            wall_chunk(src, dst, c, False, tuple(range(1, rtiles - 1)))
         else:
-            pl.when(t < SUBSTEPS)(send)
-
-            @pl.when(t == SUBSTEPS)
-            def _():
-                for k in range(wt):
-                    store_wall(c, k).start()
-
-    def two_steps(u, carry):
-        for odd, src, dst in ((1, A, B), (0, B, A)):
-
-            def body(i, inner_carry, odd=odd, src=src, dst=dst):
-                step(src, dst, u, odd, i)
-                return inner_carry
-
-            lax.fori_loop(0, chunks, body, 0)
-        return carry
-
-    lax.fori_loop(0, SUBSTEPS // 2, two_steps, 0)
-
-    for r in range(strip // SUB):
-        pairs = []
-        for k in range(wt):
-            base = top + 2 * r * SUB
-            x = A[0, k * CHUNK, pl.ds(base, SUB, stride=2), :] + A[0, k * CHUNK, pl.ds(base + 1, SUB, stride=2), :]
-            pairs.append(0.25 * (x + pltpu.roll(x, LANES - 1, 1)))
-        idx = (2 * lane) & (LANES - 1)
-        for k in range(gt):
-            a, b = lanes_of(pairs[2 * k], idx), lanes_of(pairs[2 * k + 1], idx)
-            WS[k, r * SUB : (r + 1) * SUB, :] = jnp.where(lane < LANES // 2, a, b)
-    self_tile = (gz == 0) & (gy == 0)
-
-    @pl.when(jnp.logical_not(self_tile))
-    def _():
-        wt_copy().start()
-
-    @pl.when(self_tile)
-    def _():
-        WR[:, 0:strip, :] = WS[...]
+            wall_chunk(src, dst, c, True, tuple(range(rtiles)))
+            pl.when(c == 0)(wall_mean)
+
+    for t in range(1, SUBSTEPS + 1):
+        src, dst = (A, B) if t % 2 else (B, A)
+
+        def body(i, carry, src=src, dst=dst, t=t):
+            step(src, dst, t, i)
+            return carry
+
+        lax.fori_loop(0, chunks, body, 0)
 
     @pl.when(gz == 0)
     def _():
@@ -723,8 +772,6 @@
             gap = jnp.where(FL[:, cs] == 1, 2.0 * (WR[k] - G[0, 1, k, top : top + rows_g, :]), 0.0)
             TO[0, :, cs] = TO[0, :, cs] + TIME_STEP * (0.5 * V[0, 0, :, cs] + DIFFUSE_TEMP) * gap
 
-    store_gas(0, 0).start()
-
     @pl.when(gz == 0)
     def _():
         for copy, me, _, _ in face_pieces():
@@ -737,7 +784,8 @@
     for way in range(2):
         code_copy(way).wait_send()
         y_copy(way).wait_send()
-        zone_copy(way).wait_send()
+        for n in range(3):
+            zone_copy(way, n).wait_send()
         x_copy(way).wait_send()
         for f in range(2):
 
@@ -751,18 +799,22 @@
             first_copy(c, way).wait_send()
             for t in range(1, SUBSTEPS):
                 row_copy(t, c, way).wait_send()
-        for k in range(wt):
-            store_wall(c, k).wait()
         return carry
 
     lax.fori_loop(0, chunks, drain, 0)
 
-    def drain_gas(z, carry):
-        store_gas(0, z).wait()
-        store_gas(1, z).wait()
-        return carry
-
-    lax.fori_loop(0, layers_g, drain_gas, 0)
+
+def store_kernel(t_in, f_in, s_in, t_out, f_out, s_out, sems):
+    copies = []
+    for n, (src, dst) in enumerate(((s_in, s_out), (t_in, t_out), (f_in, f_out))):
+        size = src.shape[0] // PIECES
+        for m in range(PIECES):
+            at = pl.ds(m * size, size)
+            copies.append(pltpu.make_async_copy(src.at[at], dst.at[at], sems.at[n, m]))
+    for copy in copies:
+        copy.start()
+    for copy in copies:
+        copy.wait()
 
 
 def shards(mesh_shape, gas_temp, fuel_frac, velocity, wall_flags, solid_temp, diffusivity, gas_owner):
@@ -773,7 +825,7 @@
     units = wt * CHUNK
     strip = rows // 2
     assert ny == nz and cols == 2 * cols_g and rows * ny == 2 * rows_g
-    assert layers_g == SUBSTEPS * chunks and 2 * layers_g <= LANES // 2 and chunks * wt >= layers_g
+    assert layers_g == 4 * chunks and chunks == SUB and 2 * layers_g <= LANES // 2
     assert wt == 2 * gt and gt == 2 and layers % CHUNK == 0
     f32, i32 = jnp.float32, jnp.int32
     dma = pltpu.SemaphoreType.DMA
@@ -784,8 +836,6 @@
         pltpu.VMEM((chunks, units + 1, rows + 2 * SUB, LANES), f32),
         pltpu.VMEM((chunks, units + 1, rows + 2 * SUB, LANES), f32),
         pltpu.VMEM((chunks, units + 1, rows, LANES), f32),
-        pltpu.VMEM((layers_g, rows_g, cols_g), f32),
-        pltpu.VMEM((layers_g, rows_g, cols_g), f32),
         pltpu.VMEM((rows, cols), i32),
         pltpu.VMEM((chunks, rows, LANES), f32),
         pltpu.VMEM((2, chunks, rows, LANES), f32),
@@ -794,26 +844,26 @@
         pltpu.VMEM((2, SUBSTEPS, chunks, units + SUB, LANES), f32),
         pltpu.VMEM((2, SUBSTEPS, chunks, units + SUB, LANES), f32),
         pltpu.VMEM((2, chunks, LANES), f32),
-        pltpu.VMEM((2, chunks, LANES), f32),
+        pltpu.VMEM((2, 3, chunks, LANES), f32),
         pltpu.VMEM((2, layers_g * 2 * gt // SUB, SUB, LANES), f32),
         pltpu.VMEM((2, layers_g * 2 * gt // SUB, SUB, LANES), f32),
         pltpu.VMEM((2, rows_g // 2, LANES), f32),
         pltpu.VMEM((2, rows_g // 2, LANES), f32),
         pltpu.VMEM((gt, rows_g, LANES), f32),
-        pltpu.VMEM((gt + 2, strip + 2 * SUB, LANES), f32),
-        pltpu.VMEM((wt, 2 * (strip + 2 * SUB), LANES), f32),
+        pltpu.VMEM((gt + 2, strip + 2 * DISP, LANES), f32),
+        pltpu.VMEM((wt, 2 * (strip + 2 * DISP), LANES), f32),
         pltpu.VMEM((wt + 1, rows, LANES), f32),
+        pltpu.VMEM((wt, rows, LANES), f32),
         pltpu.VMEM((gt, strip, LANES), f32),
         pltpu.VMEM((gt, rows_g, LANES), f32),
         dma((chunks, wt)),
         dma((chunks, wt)),
         dma((2, gt)),
-        dma((3,)),
-        dma((3, chunks, wt)),
+        dma((3 + gt,)),
         dma((2, SUBSTEPS, chunks)),
         dma((2, SUBSTEPS, chunks)),
-        dma((2,)),
-        dma((2,)),
+        dma((2, 3)),
+        dma((2, 3)),
         dma((2, chunks)),
         dma((2, chunks)),
         dma((2,)),
@@ -829,20 +879,27 @@
         dma(()),
         dma((ny,)),
     ]
-    return pl.pallas_call(
+    shapes = (gas_temp.shape, fuel_frac.shape, solid_temp.shape)
+    held = pl.pallas_call(
         functools.partial(mega_kernel, mesh_shape),
-        out_shape=(
-            jax.ShapeDtypeStruct(gas_temp.shape, f32),
-            jax.ShapeDtypeStruct(fuel_frac.shape, f32),
-            jax.ShapeDtypeStruct(solid_temp.shape, f32),
-        ),
+        out_shape=tuple(pltpu.VMEM(shape, f32) for shape in shapes),
         in_specs=[ANY] * 7,
-        out_specs=(ANY,) * 3,
+        out_specs=(VMEM,) * 3,
         scratch_shapes=scratch,
-        compiler_params=pltpu.CompilerParams(vmem_limit_bytes=60 << 20, has_side_effects=True),
+        compiler_params=pltpu.CompilerParams(vmem_limit_bytes=50 << 20, has_side_effects=True, collective_id=0),
         cost_estimate=pl.CostEstimate(flops=200_000_000, bytes_accessed=26 << 20, transcendentals=1 << 19),
         name="section",
     )(gas_temp, fuel_frac, velocity, wall_flags, solid_temp, diffusivity, gas_owner)
+    return pl.pallas_call(
+        store_kernel,
+        out_shape=tuple(jax.ShapeDtypeStruct(shape, f32) for shape in shapes),
+        in_specs=[VMEM] * 3,
+        out_specs=(ANY,) * 3,
+        scratch_shapes=[dma((3, PIECES))],
+        compiler_params=pltpu.CompilerParams(vmem_limit_bytes=1 << 20),
+        cost_estimate=pl.CostEstimate(flops=0, bytes_accessed=16 << 20, transcendentals=0),
+        name="store",
+    )(*held)
 
 
 def solution(mesh):

time: 63.2 us -> 48.7 us (0.77)
  local copies, waits for them, and re-layouts: 8.24 us -> 0 us
  Pallas kernels: 54.2 us -> 47.9 us
    unnamed x7 -> x0, local copies, waits for them, and re-layouts: 8.24 us -> none
    pallas_call x1 -> x2, Pallas kernels: 54.2 us -> 47.9 us  [the longest x1 44.5 us: shards(): pl.pallas_call(functools.partial(mega_kernel, mesh_shape), out_shape=tupl...]
where the time goes in v2:
time: 48.7 us; the launch traced here: 48.5 us
  Pallas kernels  47.9 us (98%)
  between operations  0.64 us (1%)
    pallas_call x1, Pallas kernels, shards(): pl.pallas_call(functools.partial(mega_kernel, mesh_shape), out_shape=tupl...  44.5 us
    pallas_call x1, Pallas kernels, shards(): pl.pallas_call(store_kernel, out_shape=tuple((jax.ShapeDtypeStruct(shape,...  3.38 us

profile of v2, /device:TPU:0, one launch (start us, length us, event | category | flops | bytes accessed | tf_op | source)
XLA Modules:
  0.0 48.5 jit_solution(18266918340947934205)
XLA Ops:
  0.6 44.5 %section.1 = (f32[32,64,256]{2,1,0:T(8,128)S(1)}, f32[32,64,256]{2,1,0:T(8,128)S(1)}, f32[64,32,512]{2,1,0:T(8,128)S(1)}) custom-call(f32[32,64,256]{2,1,0:T(8,128)} %temp_in.1, f32[32,64,256]{2,1,0:T(8,128)} %fuel_in.1, f32[3,32,64,256]{3,2,1,0:T(8,128)} %vel_in.1, s32[64,256]{1,0:T(8,128)} %flags_in.1, f32[64,32,512]{2,1,0:T(8,128)} %solid_in.1, ...), custom_call_target="tpu_custom_call" | custom-call | flops 200000000 | bytes 27262976 | tf_op jit(solution)/shard_map/section/pallas_call | solution.py:883
  45.2 3.4 %store.1 = (f32[32,64,256]{2,1,0:T(8,128)}, f32[32,64,256]{2,1,0:T(8,128)}, f32[64,32,512]{2,1,0:T(8,128)}) custom-call(f32[32,64,256]{2,1,0:T(8,128)S(1)} %get-tuple-element.6.t_in, f32[32,64,256]{2,1,0:T(8,128)S(1)} %get-tuple-element.7.f_in, f32[64,32,512]{2,1,0:T(8,128)S(1)} %get-tuple-element.8.s_in), custom_call_target="tpu_custom_call" | custom-call | bytes 16777216 | tf_op jit(solution)/shard_map/store/pallas_call | solution.py:893
